TPU v7x, 128 devices: a whole 4x4x4 slice. The times are simulated.
128 devices in a mesh: seq: 16 (over z, y), mp: 8 (over x, core).
Axes of the slice: x: 4, y: 4, z: 4, core: 2. Of those that a mesh axis runs over, the one named last changes fastest.
Arguments:
- resid: bfloat16 [4096, 5120], P('seq', 'mp'), may hold values from -15 to 15
- queries: bfloat16 [4096, 5120], P('seq', 'mp'), may hold values from -28 to 28
- keys: bfloat16 [4096, 5120], P('seq', 'mp'), may hold values from -12.25 to 12.25
- values: bfloat16 [4096, 5120], P('seq', 'mp'), may hold values from -6 to 6
- doc_ids: int32 [4096], P('seq'), may hold values from 0 to 3, as said below
- out_proj: bfloat16 [5120, 5120], P('mp'), may hold values from -0.5 to 0.5
- ffn_gain: bfloat16 [5120], P('mp'), may hold values from 0.25 to 1.75
- w_in: bfloat16 [5120, 13824], P('mp', 'seq'), may hold values from -0.078125 to 0.078125
- w_out: bfloat16 [13824, 5120], P('seq', 'mp'), may hold values from -0.109375 to 0.109375
- hot_index: int32 [16, 384], P('seq'), may hold values from 0 to 863, as said below
- hot_blocks: int32 [16], P('seq'), may hold values from 1 to 3, as said below
Outputs:
- layer_out: bfloat16 [4096, 5120], P('seq', 'mp')
- hot_mean: float32 [16, 384], P('seq')
Inputs may be any that keep to these rules, and one draw needn't show every extreme that they name: `doc_ids`: document numbers never fall along the tokens; every number from 0 to 3 occurs; some document has 2048 tokens. `hot_index`: row g holds 384 distinct neuron numbers of group g; only its first 128 * hot_blocks[g] entries are live, the others are ignored. `hot_blocks`: some group has exactly 3 live blocks.
All inputs are finite; a program needn't handle non-finite values.
Results may differ from a plain program's by a relative error of at most 0.014.
Values may be sent and summed in bfloat16 or wider, within the bound.
A program may use at most 192 MiB of HBM per device.

v0:
```python
import jax
import jax.numpy as jnp
from jax import lax
from jax.sharding import PartitionSpec as P

D = 5120
HEAD_DIM = 128
BLOCK = 128


epsilon = 1e-05
masked_score = -1e30


def copy_for_each(value, axis):
    length = lax.axis_size(axis)
    return lax.all_to_all(
        jnp.broadcast_to(value[None], (length, *value.shape)), axis, 0, 0, tiled=True
    )


def over_copies(value, axis):
    everything = copy_for_each(value, axis)
    return jnp.sum(everything, axis=0)


def joined_along(blocks, dim):
    dims = list(blocks.shape[1:])
    dims[dim] *= blocks.shape[0]
    return jnp.moveaxis(blocks, 0, dim).reshape(dims)


def one_gather(arrays, axis, dims):
    line = jnp.concatenate([a.reshape(-1) for a in arrays])
    lines, at, outs = (lax.all_gather(line, axis), 0, [])
    for a, dim in zip(arrays, dims):
        blocks = lines[:, at : at + a.size].reshape(-1, *a.shape)
        outs.append(joined_along(blocks, dim))
        at += a.size
    return tuple(outs)


def side_by_side(arrays, axis, dim, along):
    both = jnp.concatenate(arrays, axis=along)
    out, at, outs = (lax.all_gather(both, axis, axis=dim, tiled=True), 0, [])
    for a in arrays:
        outs.append(lax.slice_in_dim(out, at, at + a.shape[along], axis=along))
        at += a.shape[along]
    return tuple(outs)


def split_up(value, dim, length):
    before, after = (value.shape[:dim], value.shape[dim + 1 :])
    return jnp.moveaxis(value.reshape(*before, length, -1, *after), dim, 0)


def summed_on_arrival(value, axis, dim):
    blocks = split_up(value, dim, lax.axis_size(axis))
    arrived = lax.all_to_all(blocks, axis, split_axis=0, concat_axis=0, tiled=True)
    return arrived.astype(jnp.float32).sum(axis=0)


def rows_first(arrays, axis, dims):
    turned = [jnp.moveaxis(a, dim, 0) for a, dim in zip(arrays, dims)]
    both = jnp.concatenate([t.reshape(len(t), -1) for t in turned], axis=1)
    out, at, outs = (lax.all_gather(both, axis, axis=0, tiled=True), 0, [])
    for t, dim in zip(turned, dims):
        piece = out[:, at : at + t[0].size].reshape(-1, *t.shape[1:])
        outs.append(jnp.moveaxis(piece, 0, dim))
        at += t[0].size
    return tuple(outs)


def sum_at_owner(value, axis, dim):
    blocks = split_up(value, dim, lax.axis_size(axis))
    arrived = lax.all_to_all(blocks, axis, split_axis=0, concat_axis=0, tiled=True)
    return arrived.sum(axis=0)


def attend_block(
    state, query_rows, query_pos, query_docs, key_rows, value_rows, key_pos, key_docs, scale
):
    top, total, accum = state
    scores = (
        jnp.einsum("qhd,khd->qhk", query_rows, key_rows, preferred_element_type=jnp.float32) * scale
    )
    visible = (query_pos[:, None] >= key_pos[None, :]) & (query_docs[:, None] == key_docs[None, :])
    visible = visible[:, None, :]
    scores = jnp.where(visible, scores, masked_score)
    new_top = jnp.maximum(top, jnp.max(scores, axis=2))
    weights = jnp.where(visible, jnp.exp(scores - new_top[:, :, None]), 0.0)
    total = jnp.sum(weights, axis=2)
    update = jnp.einsum(
        "qhk,khd->qhd", weights.astype(jnp.bfloat16), value_rows, preferred_element_type=jnp.float32
    )
    accum = update
    return (new_top, total, accum)


def reduce_pre(partial_pre, live):
    share = lax.psum_scatter(
        partial_pre.astype(jnp.bfloat16), "mp", scatter_dimension=0, tiled=True
    ).astype(jnp.float32)
    active = jnp.where(live[None, :], jnp.maximum(share, 0.0), 0.0)
    column_sums = over_copies(jnp.sum(active, axis=0), "mp")
    active_low = lax.all_gather(active.astype(jnp.bfloat16), "mp", axis=0, tiled=True)
    return (active_low, column_sums)


def local(
    resid, queries, keys, values, doc_ids, out_proj, ffn_gain, w_in, w_out, hot_index, hot_blocks
):
    tok_dev = resid.shape[0]
    width_dev = resid.shape[1]
    local_heads = width_dev // HEAD_DIM
    groups = lax.axis_size("seq")
    here = lax.axis_index("seq")
    total_tokens = tok_dev * groups
    scale = HEAD_DIM ** (-0.5)
    doc_table, block_table = one_gather((doc_ids, hot_blocks), "seq", (0, 0))
    positions = here * tok_dev + jnp.arange(tok_dev, dtype=jnp.int32)
    query_rows = queries.reshape(tok_dev, local_heads, HEAD_DIM)
    blocks = (query_rows, positions)
    start_state = []
    block_rows, block_pos = blocks
    count_rows = block_rows.shape[0]
    block_docs = lax.dynamic_slice_in_dim(doc_table, block_pos[0], count_rows)
    query_sets = [(block_rows, block_pos, block_docs)]
    start_state.append(
        (
            jnp.full((count_rows, local_heads), masked_score, jnp.float32),
            jnp.zeros((count_rows, local_heads), jnp.float32),
            jnp.zeros((count_rows, local_heads, HEAD_DIM), jnp.float32),
        )
    )
    start_state = tuple(start_state)
    start = jnp.int32(0)
    key_piece, value_piece = side_by_side((keys, values), "seq", 0, 1)
    count = key_piece.shape[0]
    key_rows = key_piece.reshape(count, local_heads, HEAD_DIM)
    value_rows = value_piece.reshape(count, local_heads, HEAD_DIM)
    key_pos = jnp.arange(count, dtype=jnp.int32)
    updated = []
    for fold_state, query_set in zip(start_state, query_sets):

        def visit(current, query_set=query_set):
            return attend_block(
                current,
                query_set[0],
                query_set[1],
                query_set[2],
                key_rows,
                value_rows,
                key_pos,
                doc_table,
                scale,
            )

        def keep(current):
            return current

        updated.append(lax.cond(start <= jnp.max(query_set[1]), visit, keep, fold_state))
    final = tuple(updated)
    outputs = []
    for state in final:
        count_rows = state[2].shape[0]
        outputs.append(
            (state[2] / state[1][:, :, None]).astype(jnp.bfloat16).reshape(count_rows, width_dev)
        )
    attended = outputs[0]
    projected = jnp.dot(attended, out_proj, preferred_element_type=jnp.float32)
    projected = summed_on_arrival(projected.astype(jnp.bfloat16), "mp", 1)
    state_rows = (resid.astype(jnp.float32) + projected).astype(jnp.bfloat16)
    widened = state_rows.astype(jnp.float32)
    squares = over_copies(jnp.sum(widened * widened, axis=1), "mp")
    inverse = lax.rsqrt(squares / D + epsilon)
    normed = (widened * inverse[:, None] * ffn_gain.astype(jnp.float32)).astype(jnp.bfloat16)
    chosen = hot_index[0]
    slots = chosen.shape[0]
    hot_in = jnp.take(w_in, chosen, axis=1)
    hot_out = jnp.take(w_out, chosen, axis=0)
    all_in, all_out = rows_first((hot_in, hot_out), "seq", (1, 0))
    live = (jnp.arange(slots, dtype=jnp.int32)[None, :] < BLOCK * block_table[:, None]).reshape(-1)
    partial_pre = jnp.dot(normed, all_in, preferred_element_type=jnp.float32)
    active_low, column_sums = reduce_pre(partial_pre, live)
    mean_rows = column_sums.reshape(groups, slots)
    hot_mean = sum_at_owner(mean_rows, "seq", 0) / total_tokens
    ffn_out = jnp.dot(active_low, all_out, preferred_element_type=jnp.float32)
    layer_out = (widened + ffn_out).astype(jnp.bfloat16)
    return (layer_out, hot_mean)


def solution(mesh):
    return jax.shard_map(
        local,
        mesh=mesh,
        in_specs=(
            P("seq", "mp"),
            P("seq", "mp"),
            P("seq", "mp"),
            P("seq", "mp"),
            P("seq"),
            P("mp", None),
            P("mp"),
            P("mp", "seq"),
            P("seq", "mp"),
            P("seq", None),
            P("seq"),
        ),
        out_specs=(P("seq", "mp"), P("seq", None)),
        check_vma=False,
    )
```

profile of v0, /device:TPU:1, one launch (start us, length us, event | category | flops | bytes accessed | tf_op | source)
XLA Modules:
  0.0 296.0 jit_solution(9420448367064979493)
XLA Ops:
  7.2 1.3 copy.48
  8.5 1.1 copy.49
  9.7 0.9 pad_maximum_fusion.1
  10.6 0.0 all-gather.7.cloned.1.call-start
  10.7 0.7 fusion.34
  11.4 2.2 gather_fusion
  13.7 2.2 gather_fusion.1
  15.9 0.2 broadcast_select_fusion.1
  16.1 1.0 pad_maximum_fusion
  17.8 0.6 dynamic-slice
  19.1 0.1 add_dynamic-update-slice_fusion
  19.2 64.8 %all-reduce = s32[4112]{0:T(1024)S(1)} all-reduce(s32[4112]{0:T(1024)S(1)} %add_dynamic-update-slice_fusion), channel_id=2, replica_groups=mesh['seq'=16,'mp'=8] {'seq'}, use_global_device_ids=true, to_apply=%add | all-reduce | flops 4112 | bytes 32896
  84.0 0.1 reshape.186
  84.1 0.6 fusion.35
  85.4 15.6 %all-gather.5.cloned.1.call-done = bf16[4096,1280]{0,1:T(8,128)(2,1)} async-done(((bf16[256,1280]{0,1:T(8,128)(2,1)}), bf16[4096,1280]{0,1:T(8,128)(2,1)}) %all-gather.5.cloned.1.call-update) | async-done | bytes 10485776 | tf_op jit(solution)/shard_map/all_gather | solution.py:45
  101.0 50.6 %conditional.1 = (f32[256,5]{0,1:T(8,128)S(1)}, f32[256,5,128]{0,2,1:T(8,128)S(1)}) conditional(s32[]{:T(128)} %convert_element_type.45, () %tuple.24, (s32[256]{0:T(256)S(1)}, s32[4096]{0:T(1024)S(1)}, s32[16,257]{1,0:T(8,128)S(1)}, bf16[4096,1280]{0,1:T(8,128)(2,1)}, bf16[256,640]{1,0:T(8,128)(2,1)S(1)}) %tuple.48), branch_computations={%region_1.0_spmd, %region_2.5_spmd} | conditional | flops 2755656448 | bytes 101648448 | solution.py:162
  101.0 0.5 slice.25
  103.5 0.1 dynamic_slice.5
  103.5 1.4 compare_and_fusion
  104.9 9.7 %fusion.36 = (bf16[4096,640]{0,1:T(8,128)(2,1)}, bf16[4096,640]{0,1:T(8,128)(2,1)}) fusion(bf16[4096,1280]{0,1:T(8,128)(2,1)} %get-tuple-element.71), kind=kLoop, calls=%fused_computation.55 | loop fusion | bytes 20971520 | tf_op jit(solution)/shard_map/slice | solution.py:47
  114.7 0.2 copy.50
  114.9 12.8 %fusion = (f32[256,5]{0,1:T(8,128)S(1)}, f32[5,4096,256]{2,1,0:T(8,128)}) fusion(pred[256,4096]{0,1:T(8,128)(4,1)S(1)} %compare_and_fusion, bf16[4096,5,128]{0,2,1:T(8,128)(2,1)} %bitcast.40, bf16[256,5,128]{0,2,1:T(8,128)(2,1)S(1)} %bitcast.45), kind=kOutput, calls=%fused_computation.4 | convolution fusion | flops 1357904640 | bytes 27595776 | tf_op jit(solution)/shard_map/cond/branch_1_fun/qhd,khd->qhk/dot_general | solution.py:85
  127.7 12.9 %fusion.6 = f32[256,5,128]{2,0,1:T(8,128)S(1)} fusion(bf16[4096,5,128]{0,2,1:T(8,128)(2,1)} %bitcast.43, f32[5,4096,256]{2,1,0:T(8,128)} %get-tuple-element.107, f32[256,5]{0,1:T(8,128)S(1)} %broadcast_maximum_fusion, pred[256,4096]{0,1:T(8,128)(4,1)S(1)} %compare_and_fusion), kind=kOutput, calls=%fused_computation.10 | convolution fusion | flops 1368391680 | bytes 27923456 | tf_op jit(solution)/shard_map/cond/branch_1_fun/qhk,khd->qhd/dot_general | solution.py:93
  140.6 0.2 copy.61
  140.9 10.7 %fusion.2 = f32[256,5]{0,1:T(8,128)S(1)} fusion(f32[5,4096,256]{2,1,0:T(8,128)} %get-tuple-element.107, f32[256,5]{0,1:T(8,128)S(1)} %broadcast_maximum_fusion, pred[256,4096]{0,1:T(8,128)(4,1)S(1)} %compare_and_fusion), kind=kLoop, calls=%fused_computation.6 | loop fusion | flops 26213120 | bytes 22030336 | tf_op jit(solution)/shard_map/cond/branch_1_fun/reduce_sum | solution.py:92
  151.5 0.1 divide_convert_fusion
  151.6 5.4 %convolution_convert_fusion = bf16[256,5120]{1,0:T(8,128)(2,1)S(1)} fusion(bf16[256,640]{0,1:T(8,128)(2,1)S(1)} %bitcast.44, bf16[640,5120]{1,0:T(8,128)(2,1)} %param.18), kind=kOutput, calls=%fused_computation.21 | convolution fusion | flops 1679032320 | bytes 9502720 | tf_op jit(solution)/shard_map/dot_general | solution.py:171
  157.0 0.2 copy.68
  157.2 38.2 %all_to_all.22 = bf16[8,256,640]{2,1,0:T(8,128)(2,1)S(1)} all-to-all(bf16[8,256,640]{2,1,0:T(8,128)(2,1)S(1)} %bitcast.41), channel_id=1, replica_groups=mesh['seq'=16,'mp'=8] {'mp'}, dimensions={0} | all-to-all | bytes 5242880 | tf_op jit(solution)/shard_map/all_to_all | solution.py:59
  195.5 0.3 convert_reduce_fusion
  195.8 0.2 fusion.27
  196.0 0.6 broadcast_in_dim.86
  196.6 4.2 %all-to-all-start.1 = ((f32[8,1,256]{2,1,0:T(1,128)}), f32[8,1,256]{2,1,0:T(1,128)S(1)}, u32[]{:S(2)}, u32[]{:S(2)}) async-start(f32[8,1,256]{2,1,0:T(1,128)} %broadcast_in_dim.86), calls=%async_computation.1 | async-start | bytes 16384 | tf_op jit(solution)/shard_map/all_to_all | solution.py:17
  200.9 4.7 %all-to-all-done.1 = f32[8,1,256]{2,1,0:T(1,128)S(1)} async-done(((f32[8,1,256]{2,1,0:T(1,128)}), f32[8,1,256]{2,1,0:T(1,128)S(1)}, u32[]{:S(2)}, u32[]{:S(2)}) %all-to-all-start.1) | async-done | bytes 8224 | tf_op jit(solution)/shard_map/all_to_all | solution.py:17
  205.6 4.0 %all-gather.7.cloned.1.call-done = bf16[6144,1280]{1,0:T(8,128)(2,1)} async-done(((bf16[384,1280]{1,0:T(8,128)(2,1)}), bf16[6144,1280]{1,0:T(8,128)(2,1)}) %all-gather.7.cloned.1.call-update) | async-done | bytes 15728656 | tf_op jit(solution)/shard_map/all_gather | solution.py:66
  209.7 7.6 %fusion.16 = bf16[256,6144]{1,0:T(8,128)(2,1)} fusion(bf16[6144,1280]{1,0:T(8,128)(2,1)} %all-gather.7.cloned.1.call-done, bf16[256,640]{1,0:T(8,128)(2,1)S(1)} %get-tuple-element.103, f32[640]{0:T(1024)S(1)} %convert_element_type.51, f32[256]{0:T(256)S(1)} %add_rsqrt_fusion), kind=kOutput, calls=%fused_computation.20 | convolution fusion | flops 2015494144 | bytes 11341312 | tf_op jit(solution)/shard_map/dot_general | solution.py:184
  217.2 0.0 all-gather.9.cloned.1.call-start
  217.3 0.1 fusion.33
  217.4 0.1 iota_compare_fusion
  217.5 32.6 %reduce-scatter.2.cloned.1.call-done = bf16[32,6144]{1,0:T(8,128)(2,1)} async-done(((bf16[256,6144]{1,0:T(8,128)(2,1)}), bf16[32,6144]{1,0:T(8,128)(2,1)}) %reduce-scatter.2.cloned.1.call-update) | async-done | bytes 393232 | tf_op jit(solution)/shard_map/reduce_scatter | solution.py:101
  250.1 1.9 fusion.25
  252.0 0.1 broadcast_in_dim.91
  252.1 11.8 %all_to_all.23 = f32[8,1,6144]{2,1,0:T(1,128)S(1)} all-to-all(f32[8,1,6144]{2,1,0:T(1,128)S(1)} %broadcast_in_dim.91), channel_id=1, replica_groups=mesh['seq'=16,'mp'=8] {'mp'}, dimensions={0} | all-to-all | bytes 393216 | tf_op jit(solution)/shard_map/all_to_all | solution.py:17
  263.9 0.1 reduce_sum.69
  264.1 12.9 %all_to_all.24 = f32[16,1,384]{2,1,0:T(1,128)S(1)} all-to-all(f32[16,1,384]{2,1,0:T(1,128)S(1)} %bitcast.46), channel_id=1, replica_groups=mesh['seq'=16,'mp'=8] {'seq'}, dimensions={0} | all-to-all | bytes 49152 | tf_op jit(solution)/shard_map/all_to_all | solution.py:76
  277.1 0.6 div.28
  277.6 4.3 %all-gather.9.cloned.1.call-done = bf16[256,6144]{1,0:T(8,128)(2,1)} async-done(((bf16[32,6144]{1,0:T(8,128)(2,1)}), bf16[256,6144]{1,0:T(8,128)(2,1)}) %all-gather.9.cloned.1.call-update) | async-done | bytes 3145744 | tf_op jit(solution)/shard_map/all_gather | solution.py:106
  281.9 7.5 %fusion.22 = bf16[256,640]{1,0:T(8,128)(2,1)} fusion(bf16[256,6144]{1,0:T(8,128)(2,1)} %all-gather.9.cloned.1.call-done, bf16[6144,1280]{1,0:T(8,128)(2,1)} %all-gather.7.cloned.1.call-done, bf16[256,640]{1,0:T(8,128)(2,1)S(1)} %get-tuple-element.103), kind=kOutput, calls=%fused_computation.25 | convolution fusion | flops 2013757440 | bytes 11665408 | tf_op jit(solution)/shard_map/dot_general | solution.py:188
  (39 shorter events, 0.3 us)
Async XLA Ops:
  7.2 4.2 %copy-start = (bf16[640,864]{0,1:T(8,128)(2,1)S(1)}, bf16[640,864]{0,1:T(8,128)(2,1)}, u32[]{:S(2)}) copy-start(bf16[640,864]{0,1:T(8,128)(2,1)} %param.20) | copy-start | bytes 3317764
  7.2 8.7 %copy-start.5 = (s32[1,384]{1,0:T(1,128)S(1)}, s32[1,384]{1,0:T(1,128)}, u32[]{:S(2)}) copy-start(s32[1,384]{1,0:T(1,128)} %param.22) | copy-start | bytes 4612
  7.2 6.5 %copy-start.2 = (bf16[864,640]{1,0:T(8,128)(2,1)S(1)}, bf16[864,640]{1,0:T(8,128)(2,1)}, u32[]{:S(2)}) copy-start(bf16[864,640]{1,0:T(8,128)(2,1)} %param.21) | copy-start | bytes 3317764
  7.2 93.8 %all-gather.5.cloned.1.call-start = ((), (), s32[]{:S(2)}) async-start(), calls=%async_computation.5 | async-start | bytes 11141120 | tf_op jit(solution)/shard_map/all_gather | solution.py:45
  10.6 199.0 %all-gather.7.cloned.1.call-start = ((), (), s32[]{:S(2)}) async-start(), calls=%async_computation.6 | async-start | bytes 16711680 | tf_op jit(solution)/shard_map/all_gather | solution.py:66
  11.4 6.4 %copy-start.8 = (u32[128]{0:T(128)S(1)}, u32[128]{0:T(128)}, u32[]{:S(2)}) copy-start(u32[128]{0:T(128)} %constant.82) | copy-start | bytes 1540
  11.4 7.7 %copy-start.7 = (s32[256]{0:T(256)S(1)}, s32[256]{0:T(256)}, u32[]{:S(2)}) copy-start(s32[256]{0:T(256)} %param.17) | copy-start | bytes 3076
  11.4 89.6 %copy-start.3 = (bf16[256,640]{1,0:T(8,128)(2,1)S(1)}, bf16[256,640]{1,0:T(8,128)(2,1)}, u32[]{:S(2)}) copy-start(bf16[256,640]{1,0:T(8,128)(2,1)} %param.14) | copy-start | bytes 983044
  157.0 38.9 %copy-start.4 = (bf16[256,640]{1,0:T(8,128)(2,1)S(1)}, bf16[256,640]{1,0:T(8,128)(2,1)}, u32[]{:S(2)}) copy-start(bf16[256,640]{1,0:T(8,128)(2,1)} %param.13) | copy-start | bytes 983044
  157.0 43.9 %copy-start.6 = (bf16[640]{0:T(1024)(128)(2,1)S(1)}, bf16[640]{0:T(1024)(128)(2,1)}, u32[]{:S(2)}) copy-start(bf16[640]{0:T(1024)(128)(2,1)} %param.19) | copy-start | bytes 3844
  196.6 9.0 %all-to-all-start.1 = ((f32[8,1,256]{2,1,0:T(1,128)}), f32[8,1,256]{2,1,0:T(1,128)S(1)}, u32[]{:S(2)}, u32[]{:S(2)}) async-start(f32[8,1,256]{2,1,0:T(1,128)} %broadcast_in_dim.86), calls=%async_computation.1 | async-start | bytes 16384 | tf_op jit(solution)/shard_map/all_to_all | solution.py:17
  200.8 49.3 %reduce-scatter.2.cloned.1.call-start = ((), (), s32[]{:S(2)}) async-start(), calls=%async_computation.7 | async-start | bytes 3538944 | tf_op jit(solution)/shard_map/reduce_scatter | solution.py:101
  217.2 64.7 %all-gather.9.cloned.1.call-start = ((), (), s32[]{:S(2)}) async-start(), calls=%async_computation.8 | async-start | bytes 3538944 | tf_op jit(solution)/shard_map/all_gather | solution.py:106
  277.1 12.4 %copy-start.1 = (bf16[640,864]{0,1:T(8,128)(2,1)S(1)}, bf16[640,864]{0,1:T(8,128)(2,1)}, u32[]{:S(2)}) copy-start(bf16[640,864]{0,1:T(8,128)(2,1)} %param.20) | copy-start | bytes 3317764
Sparse Core Ops, SparseCore 0:
  10.7 90.1 all-gather.4
  103.1 106.5 all-gather.6
  217.4 32.6 reduce-scatter.1
  252.1 29.8 all-gather.8
where the time goes:
time: 297 us; the launch traced here: 296 us
  blocking collectives  128 us (43%)
  waiting for transfers between devices  61.3 us (21%)
  matrix products  46.2 us (16%)
  local copies, waits for them, and re-layouts  19.9 us (7%)
  other arithmetic  18.6 us (6%)
  between operations  16 us (5%)
  starting transfers between devices  4.34 us (1%)
    unnamed x1, blocking collectives  64.8 us
    all_to_all x1, blocking collectives, summed_on_arrival(): lax.all_to_all(blocks, axis, split_axis=0, concat_axis=0, tiled=True)  38.2 us
    reduce_scatter x1, waiting for transfers between devices, reduce_pre(): lax.psum_scatter(partial_pre.astype(jnp.bfloat16), 'mp', scatter_dimensio...  32.6 us
    all_gather x1, waiting for transfers between devices, side_by_side(): out, at, outs = (lax.all_gather(both, axis, axis=dim, tiled=True), 0, [])  15.6 us
    all_to_all x1, blocking collectives, sum_at_owner(): lax.all_to_all(blocks, axis, split_axis=0, concat_axis=0, tiled=True)  12.9 us
    dot_general x1, matrix products, attend_block(): jnp.einsum('qhk,khd->qhd', weights.astype(jnp.bfloat16), value_rows, pref...  12.9 us
    dot_general x1, matrix products, attend_block(): jnp.einsum('qhd,khd->qhk', query_rows, key_rows, preferred_element_type=j...  12.8 us
    all_to_all x1, blocking collectives, copy_for_each(): lax.all_to_all(jnp.broadcast_to(value[None], (length, *value.shape)), axi...  11.8 us
  transfers between devices with their start and end apart: 5, of which 5 were waited for; matrix products, arithmetic and copies ran while one was open for 22% of the time, Pallas kernels for 0%

commit v1 on v0

v1 whole, which is shorter than its diff:
```python
import jax
import jax.numpy as jnp
from jax import lax
from jax.experimental import pallas as pl
from jax.experimental.pallas import tpu as pltpu
from jax.sharding import PartitionSpec as P

HEAD_DIM = 128
HEADS = 5
TOK = 256
WID = 640
SLOTS = 384
BLOCK = 128
NEUR = 864
D = 5120
TOKENS = 4096
EPS = 1e-05
LOW = -1e9
MASKED = -2e9
SCALE2 = HEAD_DIM ** (-0.5) * 1.4426950408889634
BF = jnp.bfloat16
F32 = jnp.float32
ORDER = (1, 3, 2)


def dot(a, b, dims):
    return lax.dot_general(a, b, (dims, ((), ())), preferred_element_type=F32)


def kernel(
    q_ref, k_ref, v_ref, resid_ref, doc_ref, oproj_ref, gain_ref, win_ref, wout_ref, hidx_ref,
    hblk_ref, out_ref, hm_ref,
    qb, kb, vb, drow, qrow, kcol, accw, acc0, st0, osend, ssend, orecv, srecv, att, wo, res,
    psend, precv, wi_own, wo_own, hin, win, wou, sqs, nb, prebuf, presend, prerecv, ab, fown,
    fsend, frecv, csum, csr, hs, hsr,
    kv_s, kv_r, q_s, q_r, d_s, d_r, o_s, o_r, a_s, a_r, wo_s, wo_r, wo_l, p_s, p_r, l_s, own_l,
    wi_s, wi_r, wu_s, wu_r, sq_s, sq_r, n_s, n_r, nd_s, nd_r, rs_s, rs_r, ag_s, ag_r, ad_s, ad_r,
    f_s, f_r, c_s, c_r, h_s, h_r,
):
    s = lax.axis_index("seq")
    m = lax.axis_index("mp")
    z, y, x, c = s // 4, s % 4, m // 2, m % 2

    def dev(dz=0, dy=0, dx=0, dc=0):
        return (((z + dz) % 4) * 4 + (y + dy) % 4, ((x + dx) % 4) * 2 + (c + dc) % 2)

    def remote(src, dst, ss, rs, device):
        return pltpu.make_async_remote_copy(
            src_ref=src, dst_ref=dst, send_sem=ss, recv_sem=rs, device_id=device,
            device_id_type=pl.DeviceIdType.MESH,
        )

    peer = dev(dc=1)
    sent = []

    def go(cp):
        cp.start()
        sent.append(cp)
        return cp

    def lane(ref, h):
        return ref.at[:, h * HEAD_DIM : (h + 1) * HEAD_DIM]

    loads = []
    for h in range(HEADS):
        for j, (src, dst) in enumerate(((q_ref, qb), (k_ref, kb), (v_ref, vb))):
            cp = pltpu.make_async_copy(lane(src, h), dst.at[0, h], own_l.at[j, h])
            cp.start()
            loads.append(cp)
    big = [
        pltpu.make_async_copy(win_ref, wi_own, l_s.at[0]),
        pltpu.make_async_copy(wout_ref, wo_own, l_s.at[1]),
        pltpu.make_async_copy(resid_ref, res, l_s.at[2]),
    ]
    for cp in big:
        cp.start()

    barrier = pltpu.get_barrier_semaphore()
    friends = [peer]
    for r in (1, 2, 3):
        friends += [dev(dy=r), dev(dy=r, dc=1), dev(dz=r), dev(dx=r), dev(dx=r, dc=1)]
    for f in friends:
        pl.semaphore_signal(barrier, inc=1, device_id=f, device_id_type=pl.DeviceIdType.MESH)
    doc_here = jnp.broadcast_to(doc_ref[...].astype(F32), (8, TOK))
    drow[0] = doc_here
    qrow[0] = doc_here
    pl.semaphore_wait(barrier, len(friends))

    doc_in = []
    for r in (1, 2, 3):
        doc_in.append(go(remote(drow.at[0], drow.at[r], d_s.at[r], d_r.at[r], dev(dy=r))))
    for r in (1, 2):
        doc_in.append(go(remote(drow.at[0], qrow.at[r], d_s.at[3 + r], d_r.at[3 + r], dev(dz=-r))))
    for h in range(HEADS):
        for r in ORDER:
            go(remote(lane(k_ref, h), kb.at[r, h], kv_s.at[0, r, h], kv_r.at[0, r, h], dev(dy=r)))
            go(remote(lane(v_ref, h), vb.at[r, h], kv_s.at[1, r, h], kv_r.at[1, r, h], dev(dy=r)))
        for r in (1, 2):
            go(remote(lane(q_ref, h), qb.at[r, h], q_s.at[r, h], q_r.at[r, h], dev(dz=-r)))

    wo_loc, wo_rem = [], []
    rows_c = pl.ds(pl.multiple_of(c * WID, 128), WID)
    for d in range(4):
        mine = pl.ds(pl.multiple_of((2 * d + c) * WID, 128), WID)
        theirs = pl.ds(pl.multiple_of((2 * d + 1 - c) * WID, 128), WID)
        cp = pltpu.make_async_copy(oproj_ref.at[:, mine], wo.at[d, rows_c, :], wo_l.at[d])
        cp.start()
        wo_loc.append(cp)
        wo_rem.append(
            go(remote(oproj_ref.at[:, theirs], wo.at[d, rows_c, :], wo_s.at[d], wo_r.at[d], peer))
        )

    for cp in big:
        cp.wait()
    live = lax.broadcasted_iota(jnp.int32, (1, SLOTS), 1) < BLOCK * hblk_ref[0]
    want = jnp.where(live, hidx_ref[...], -1)
    pick = (lax.broadcasted_iota(jnp.int32, (NEUR, SLOTS), 0) == want).astype(F32).astype(BF)
    hin[...] = dot(wi_own[...], pick, ((1,), (0,))).astype(BF)
    my_rows = pl.ds(pl.multiple_of(y * SLOTS, 128), SLOTS)
    wou[my_rows, :] = dot(pick, wo_own[...], ((0,), (0,))).astype(BF)
    ct = y // 2
    win_dst = win.at[rows_c, pl.ds(pl.multiple_of((y % 2) * SLOTS, 128), SLOTS)]

    @pl.when(ct == c)
    def _():
        win[rows_c, pl.ds(pl.multiple_of((y % 2) * SLOTS, 128), SLOTS)] = hin[...]

    wi_peer = remote(hin, win_dst, wi_s.at[0], wi_r.at[y % 2, c], peer)

    @pl.when(ct != c)
    def _():
        wi_peer.start()

    wu_in = []
    for r in ORDER:
        go(
            remote(
                hin, win_dst, wi_s.at[r], wi_r.at[y % 2, c],
                (z * 4 + (y + r) % 4, 2 * x + ct),
            )
        )
        wu_in.append(
            go(remote(wou.at[my_rows], wou.at[my_rows], wu_s.at[r], wu_r.at[r], dev(dy=r)))
        )

    for cp in loads:
        cp.wait()
    for cp in doc_in:
        cp.wait_recv()
    for r in range(4):
        kcol[r] = jnp.transpose(jnp.broadcast_to(drow[r][0:1, :], (128, TOK)))

    def step(h, i, r, qd, top, total, causal):
        sc = dot(kb[r, h], qb[i, h], ((1,), (1,)))
        kd = kcol[r]
        mask = jnp.concatenate([kd, kd], axis=1) == qd
        if causal:
            key_at = lax.broadcasted_iota(jnp.int32, (TOK, TOK), 0)
            query_at = lax.broadcasted_iota(jnp.int32, (TOK, TOK), 1)
            mask = mask & (key_at <= query_at)
        sc = jnp.where(mask, sc, MASKED)
        new = jnp.maximum(top, jnp.max(sc, axis=0, keepdims=True))
        p = jnp.exp2((sc - new) * SCALE2)
        fade = jnp.exp2((top - new) * SCALE2)
        total = total * fade + jnp.sum(p, axis=0, keepdims=True)
        accw[...] = accw[...] * fade + dot(vb[r, h], p.astype(BF), ((0,), (0,)))
        return new, total

    low = jnp.full((1, TOK), LOW, F32)
    zero = jnp.zeros((1, TOK), F32)

    def both(top, total):
        row = lax.broadcasted_iota(jnp.int32, (8, TOK), 0)
        return jnp.where(row == 0, top, total)

    def back(i, h):
        return (
            remote(
                osend.at[i - 1, h], orecv.at[i - 1, h], o_s.at[0, i - 1, h], o_r.at[0, i - 1, h],
                (((z + i) % 4) * 4 + y, m),
            ),
            remote(
                ssend.at[i - 1, h], srecv.at[i - 1, h], o_s.at[1, i - 1, h], o_r.at[1, i - 1, h],
                (((z + i) % 4) * 4 + y, m),
            ),
        )

    def head(h, _):
        for r in (1, 2):
            remote(qb.at[0, h], qb.at[r, h], q_s.at[r, h], q_r.at[r, h], dev(dz=-r)).wait_recv()
        for r in ORDER:
            remote(kb.at[0, h], kb.at[r, h], kv_s.at[0, r, h], kv_r.at[0, r, h], peer).wait_recv()
            remote(vb.at[0, h], vb.at[r, h], kv_s.at[1, r, h], kv_r.at[1, r, h], peer).wait_recv()

        def away(t, _):
            i = 2 - t
            qd = jnp.where(z + i <= 3, qrow[i][0:1, :], -5.0)
            accw[...] = jnp.zeros_like(accw)

            def visit(n, carry):
                r = jnp.where(jnp.logical_and(i == 2, n > 0), y + n, n)
                return step(h, i, r, qd, *carry, False)

            top, total = lax.fori_loop(0, jnp.where(i == 2, 4 - y, 4), visit, (low, zero))
            osend[i - 1, h] = accw[...].astype(BF)
            ssend[i - 1, h] = both(top, total)
            for cp in back(i, h):
                cp.start()
            return 0

        lax.fori_loop(0, 2, away, 0)
        accw[...] = jnp.zeros_like(accw)
        qd = qrow[0][0:1, :]
        carry = step(h, 0, 0, qd, low, zero, True)
        top, total = lax.fori_loop(
            1, y + 1, lambda r, carry: step(h, 0, r, qd, *carry, False), carry
        )
        acc0[h] = accw[...]
        st0[h] = both(top, total)
        return 0

    lax.fori_loop(0, HEADS, head, 0)

    def swap(h):
        return remote(att.at[c, h], att.at[c, h], a_s.at[h], a_r.at[h], peer)

    def merge(h, _):
        for i in (1, 2):
            for cp in back(i, h):
                cp.wait_recv()
        t0, t1, t2 = st0[h][0:1, :], srecv[0, h][0:1, :], srecv[1, h][0:1, :]
        n0, n1, n2 = st0[h][1:2, :], srecv[0, h][1:2, :], srecv[1, h][1:2, :]
        top = jnp.maximum(t0, jnp.maximum(t1, t2))
        f0 = jnp.exp2((t0 - top) * SCALE2)
        f1 = jnp.exp2((t1 - top) * SCALE2)
        f2 = jnp.exp2((t2 - top) * SCALE2)
        inv = 1.0 / (n0 * f0 + n1 * f1 + n2 * f2)
        mixed = (
            acc0[h] * (f0 * inv)
            + orecv[0, h].astype(F32) * (f1 * inv)
            + orecv[1, h].astype(F32) * (f2 * inv)
        )
        att[c, h] = jnp.transpose(mixed).astype(BF)
        swap(h).start()
        return 0

    lax.fori_loop(0, HEADS, merge, 0)

    for cp in wo_loc:
        cp.wait()
    for cp in wo_rem:
        cp.wait_recv()
    for h in range(HEADS):
        remote(att.at[1 - c, h], att.at[1 - c, h], a_s.at[h], a_r.at[h], peer).wait_recv()
    both_att = jnp.concatenate([att[i, h] for i in (0, 1) for h in range(HEADS)], axis=1)
    p_in = []
    for r in (2, 1, 3):
        psend[r] = dot(both_att, wo[(x + r) % 4], ((1,), (0,))).astype(BF)
        p_in.append(go(remote(psend.at[r], precv.at[r], p_s.at[r], p_r.at[r], dev(dx=r))))
    fown[...] = dot(both_att, wo[x], ((1,), (0,))) + res[...].astype(F32)
    for cp in p_in:
        cp.wait_recv()
    state = (
        fown[...] + precv[1].astype(F32) + precv[2].astype(F32) + precv[3].astype(F32)
    ).astype(BF)
    res[...] = state

    wide = state.astype(F32)
    square = wide * wide
    high = square.astype(BF)
    rest = (square - high.astype(F32)).astype(BF)
    ones = jnp.ones((8, WID), BF)
    sqs[0] = dot(ones, high, ((1,), (1,))) + dot(ones, rest, ((1,), (1,)))
    sq_in = []
    for j in range(1, 8):
        cp = remote(
            sqs.at[0], sqs.at[j], sq_s.at[j], sq_r.at[j], dev(dx=j // 2, dc=j % 2)
        )
        sq_in.append(go(cp))
    for cp in sq_in:
        cp.wait_recv()
    squares = sqs[0]
    for j in range(1, 8):
        squares = squares + sqs[j]
    inverse = lax.rsqrt(squares[0:1, :] / D + EPS)
    column = jnp.transpose(jnp.broadcast_to(inverse, (128, TOK)))
    column = jnp.concatenate([column] * HEADS, axis=1)
    gain = gain_ref[...].astype(F32)
    nb[0, c] = (res[...].astype(F32) * column * gain).astype(BF)

    n_in = {}
    nd_in = {}
    nd_in[0] = go(remote(nb.at[0, c], nb.at[0, c], nd_s.at[0], nd_r.at[0], peer))
    for r in ORDER:
        n_in[r] = go(remote(nb.at[0, c], nb.at[r, c], n_s.at[r], n_r.at[r], dev(dz=r)))

    for cp in wu_in:
        cp.wait_recv()
    for gi in (0, 1):
        for cs in (0, 1):
            @pl.when(jnp.logical_not(jnp.logical_and(y == 2 * c + gi, c == cs)))
            def _():
                remote(hin, win_dst, wi_s.at[0], wi_r.at[gi, cs], peer).wait_recv()

    csum[...] = jnp.zeros_like(csum)
    rs_in, ag_in, ad_in, f_in = {}, {}, {}, {}
    my64 = pl.ds(pl.multiple_of(x * 64, 64), 64)

    def stage_a(r):
        if r:
            n_in[r].wait_recv()
            nd_in[r] = go(remote(nb.at[r, c], nb.at[r, c], nd_s.at[r], nd_r.at[r], peer))

    def stage_b(r):
        nd_in[r].wait_recv()
        rows = jnp.concatenate([nb[r, 0], nb[r, 1]], axis=1)
        pre = dot(rows, win[...], ((1,), (0,)))
        prebuf[r] = pre
        presend[r] = pre.astype(BF)
        for e in (2, 1, 3):
            there = pl.ds(pl.multiple_of(((x + e) % 4) * 64, 64), 64)
            rs_in[r, e] = go(
                remote(
                    presend.at[r, there], prerecv.at[r, e], rs_s.at[r, e], rs_r.at[r, e],
                    dev(dx=e),
                )
            )

    def stage_c(r):
        for e in (1, 3, 2):
            rs_in[r, e].wait_recv()
        pre = (
            prebuf[r, my64, :] + prerecv[r, 1].astype(F32) + prerecv[r, 2].astype(F32)
            + prerecv[r, 3].astype(F32)
        )
        active = jnp.maximum(pre, 0.0)
        csum[...] += jnp.sum(active, axis=0, keepdims=True)
        ab[r, c, my64, :] = active.astype(BF)
        for e in (2, 1, 3):
            ag_in[r, e] = go(
                remote(
                    ab.at[r, c, my64], ab.at[r, c, my64], ag_s.at[r, e], ag_r.at[r, e], dev(dx=e)
                )
            )

    def stage_d(r):
        for e in (1, 3, 2):
            ag_in[r, e].wait_recv()
        ad_in[r] = go(remote(ab.at[r, c], ab.at[r, c], ad_s.at[r], ad_r.at[r], peer))

    def stage_e(r):
        ad_in[r].wait_recv()
        rows = jnp.concatenate([ab[r, 0], ab[r, 1]], axis=1)
        part = dot(rows, wou[...], ((1,), (0,)))
        if r == 0:
            fown[...] = part
        else:
            fsend[r] = part.astype(BF)
            f_in[r] = go(remote(fsend.at[r], frecv.at[r], f_s.at[r], f_r.at[r], dev(dz=-r)))

    plan = (
        (stage_a, 0), (stage_b, 0), (stage_a, 1), (stage_b, 1), (stage_c, 0), (stage_a, 3),
        (stage_b, 3), (stage_c, 1), (stage_d, 0), (stage_a, 2), (stage_b, 2), (stage_c, 3),
        (stage_d, 1), (stage_e, 0), (stage_c, 2), (stage_d, 3), (stage_e, 1), (stage_d, 2),
        (stage_e, 3), (stage_e, 2),
    )
    for stage, r in plan:
        stage(r)

    c_in = []
    for r in (1, 2, 3):
        c_in.append(go(remote(csum, csr.at[r], c_s.at[r], c_r.at[r], dev(dx=r))))
    for cp in c_in:
        cp.wait_recv()
    sums = csum[...] + csr[1] + csr[2] + csr[3]
    h_out = []
    for gi in (0, 1):
        hs[gi] = sums[:, gi * SLOTS : (gi + 1) * SLOTS]
    for gi in (0, 1):
        for cd in (0, 1):
            cp = remote(
                hs.at[gi], hsr.at[y], h_s.at[gi, cd], h_r.at[y],
                (z * 4 + 2 * c + gi, 2 * x + cd),
            )
            mine = jnp.logical_and(y == 2 * c + gi, c == cd)
            h_out.append((cp, mine))

            @pl.when(jnp.logical_not(mine))
            def _():
                cp.start()

            @pl.when(mine)
            def _():
                hsr[y] = hs[gi]

    for r in ORDER:
        f_in[r].wait_recv()
    out_ref[...] = (
        res[...].astype(F32) + fown[...] + frecv[1].astype(F32) + frecv[2].astype(F32)
        + frecv[3].astype(F32)
    ).astype(BF)

    for src in range(4):
        @pl.when(jnp.logical_not(jnp.logical_and(src == y, y // 2 == c)))
        def _():
            remote(hs.at[0], hsr.at[src], h_s.at[0, 0], h_r.at[src], peer).wait_recv()

    hm_ref[...] = (hsr[0] + hsr[1] + hsr[2] + hsr[3])[0:1, :] / TOKENS

    for cp in sent:
        cp.wait_send()
    for cp, mine in h_out:
        @pl.when(jnp.logical_not(mine))
        def _():
            cp.wait_send()

    @pl.when(ct != c)
    def _():
        wi_peer.wait_send()

    def drain(h, _):
        for i in (1, 2):
            for cp in back(i, h):
                cp.wait_send()
        swap(h).wait_send()
        return 0

    lax.fori_loop(0, HEADS, drain, 0)


def local(resid, queries, keys, values, doc_ids, out_proj, ffn_gain, w_in, w_out, hot_index,
          hot_blocks):
    dma = pltpu.SemaphoreType.DMA
    V = pltpu.VMEM
    hbm = pl.BlockSpec(memory_space=pl.ANY)
    vm = pl.BlockSpec(memory_space=pltpu.VMEM)
    sm = pl.BlockSpec(memory_space=pltpu.SMEM)
    scratch = [
        V((3, HEADS, TOK, 128), BF), V((4, HEADS, TOK, 128), BF), V((4, HEADS, TOK, 128), BF),
        V((4, 8, TOK), F32), V((3, 8, TOK), F32), V((4, TOK, 128), F32),
        V((128, TOK), F32), V((HEADS, 128, TOK), F32), V((HEADS, 8, TOK), F32),
        V((2, HEADS, 128, TOK), BF), V((2, HEADS, 8, TOK), F32),
        V((2, HEADS, 128, TOK), BF), V((2, HEADS, 8, TOK), F32),
        V((2, HEADS, TOK, 128), BF), V((4, 2 * WID, WID), BF), V((TOK, WID), BF),
        V((4, TOK, WID), BF), V((4, TOK, WID), BF),
        V((WID, NEUR), BF), V((NEUR, WID), BF), V((WID, SLOTS), BF),
        V((2 * WID, 2 * SLOTS), BF), V((4 * SLOTS, WID), BF),
        V((8, 8, TOK), F32), V((4, 2, TOK, WID), BF), V((4, TOK, 2 * SLOTS), F32),
        V((4, TOK, 2 * SLOTS), BF), V((4, 4, 64, 2 * SLOTS), BF), V((4, 2, TOK, 2 * SLOTS), BF),
        V((TOK, WID), F32), V((4, TOK, WID), BF), V((4, TOK, WID), BF),
        V((8, 2 * SLOTS), F32), V((4, 8, 2 * SLOTS), F32), V((2, 8, SLOTS), F32),
        V((4, 8, SLOTS), F32),
        dma((2, 4, HEADS)), dma((2, 4, HEADS)), dma((3, HEADS)), dma((3, HEADS)),
        dma((6,)), dma((6,)), dma((2, 2, HEADS)), dma((2, 2, HEADS)),
        dma((HEADS,)), dma((HEADS,)), dma((4,)), dma((4,)), dma((4,)), dma((4,)), dma((4,)),
        dma((3,)), dma((3, HEADS)), dma((4,)), dma((2, 2)), dma((4,)), dma((4,)),
        dma((8,)), dma((8,)), dma((4,)), dma((4,)), dma((4,)), dma((4,)),
        dma((4, 4)), dma((4, 4)), dma((4, 4)), dma((4, 4)), dma((4,)), dma((4,)),
        dma((4,)), dma((4,)), dma((4,)), dma((4,)), dma((2, 2)), dma((4,)),
    ]
    return pl.pallas_call(
        kernel,
        out_shape=(
            jax.ShapeDtypeStruct((TOK, WID), BF), jax.ShapeDtypeStruct((1, SLOTS), F32),
        ),
        in_specs=[hbm, hbm, hbm, hbm, vm, hbm, vm, hbm, hbm, vm, sm],
        out_specs=(vm, vm),
        scratch_shapes=scratch,
        compiler_params=pltpu.CompilerParams(
            collective_id=0, has_side_effects=True, vmem_limit_bytes=60 * 2**20
        ),
        name="layer",
    )(
        queries, keys, values, resid, doc_ids.reshape(1, TOK), out_proj,
        ffn_gain.reshape(1, WID), w_in, w_out, hot_index, hot_blocks,
    )


def solution(mesh):
    return jax.shard_map(
        local,
        mesh=mesh,
        in_specs=(
            P("seq", "mp"), P("seq", "mp"), P("seq", "mp"), P("seq", "mp"), P("seq"),
            P("mp", None), P("mp"), P("mp", "seq"), P("seq", "mp"), P("seq", None), P("seq"),
        ),
        out_specs=(P("seq", "mp"), P("seq", None)),
        check_vma=False,
    )
```

time: 297 us -> 147 us (0.49)
  Pallas kernels: 0 us -> 139 us
  blocking collectives: 128 us -> 0 us
  waiting for transfers between devices: 61.3 us -> 0 us
  matrix products: 46.2 us -> 0 us
  other arithmetic: 18.6 us -> 0 us
  between operations: 16 us -> 1.29 us
  local copies, waits for them, and re-layouts: 19.9 us -> 6.65 us
  starting transfers between devices: 4.34 us -> 0 us
    pallas_call x0 -> x1, Pallas kernels: none -> 139 us  [local(): pl.pallas_call(kernel, out_shape=(jax.ShapeDtypeStruct((TOK, WID), BF), j...]
    unnamed x1 -> x0, blocking collectives: 64.8 us -> none
    all_to_all x3 -> x0, blocking collectives: 63 us -> none  [the longest x1 38.2 us: summed_on_arrival(): lax.all_to_all(blocks, axis, split_axis=0, concat_axis=0, tiled=True)]
    dot_general x5 -> x0, matrix products: 46.2 us -> none  [the longest x1 12.9 us: attend_block(): jnp.einsum('qhk,khd->qhd', weights.astype(jnp.bfloat16), value_rows, pref...]
    reduce_scatter x1 -> x0, waiting for transfers between devices: 32.6 us -> none  [reduce_pre(): lax.psum_scatter(partial_pre.astype(jnp.bfloat16), 'mp', scatter_dimensio...]
    all_gather x3 -> x0, waiting for transfers between devices: 23.9 us -> none  [the longest x1 15.6 us: side_by_side(): out, at, outs = (lax.all_gather(both, axis, axis=dim, tiled=True), 0, [])]
    reduce_sum x7 -> x0, other arithmetic: 13.3 us -> none  [the longest x1 10.7 us: attend_block(): total = jnp.sum(weights, axis=2)]
    slice x2 -> x0, local copies, waits for them, and re-layouts: 10.2 us -> none  [the longest x1 9.73 us: side_by_side(): outs.append(lax.slice_in_dim(out, at, at + a.shape[along], axis=along))]
  transfers between devices with their start and end apart: 5 -> 0, of which waited for: 5 -> 0; matrix products, arithmetic and copies ran while one was open for 22% -> 0% of each run, Pallas kernels for 0% -> 0%
where the time goes in v1:
time: 147 us
  Pallas kernels  139 us (95%)
  local copies, waits for them, and re-layouts  6.65 us (5%)
    pallas_call x1, Pallas kernels, local(): pl.pallas_call(kernel, out_shape=(jax.ShapeDtypeStruct((TOK, WID), BF), j...  139 us
    unnamed x3, local copies, waits for them, and re-layouts  5.38 us

profile of v1, /device:TPU:1, one launch (start us, length us, event | category | flops | bytes accessed | tf_op | source)
XLA Modules:
  0.0 146.6 jit_solution(12243330344299725448)
XLA Ops:
  1.3 1.3 reshape.11.gain_ref
  2.5 2.4 %copy.13.win_ref = bf16[640,864]{1,0:T(8,128)(2,1)} copy(bf16[640,864]{0,1:T(8,128)(2,1)} %param.18) | data formatting | bytes 2211840 | tf_op args[7]
  5.0 138.7 %layer.1 = (bf16[256,640]{1,0:T(8,128)(2,1)}, f32[1,384]{1,0:T(1,128)}) custom-call(bf16[256,640]{1,0:T(8,128)(2,1)} %q_ref.1, bf16[256,640]{1,0:T(8,128)(2,1)} %k_ref.1, bf16[256,640]{1,0:T(8,128)(2,1)} %v_ref.1, bf16[256,640]{1,0:T(8,128)(2,1)} %resid_ref.1, s32[1,256]{1,0:T(1,128)} %bitcast.1, bf16[640,5120]{1,0:T(8,128)(2,1)} %oproj_ref.1, ...), custom_call_target="tpu_custom_call" | custom-call | tf_op jit(solution)/shard_map/layer/pallas_call | solution.py:461
  143.6 1.7 %copy.17 = bf16[256,640]{1,0:T(8,128)(2,1)} copy(bf16[256,640]{1,0:T(8,128)(2,1)} %get-tuple-element.4) | data formatting | bytes 655360
  145.4 1.2 copy.18

commit v2 on v1

--- a/solution.py
+++ b/solution.py
@@ -31,11 +31,11 @@
     q_ref, k_ref, v_ref, resid_ref, doc_ref, oproj_ref, gain_ref, win_ref, wout_ref, hidx_ref,
     hblk_ref, out_ref, hm_ref,
     qb, kb, vb, drow, qrow, kcol, accw, acc0, st0, osend, ssend, orecv, srecv, att, wo, res,
-    psend, precv, wi_own, wo_own, hin, win, wou, sqs, nb, prebuf, presend, prerecv, ab, fown,
-    fsend, frecv, csum, csr, hs, hsr,
+    psend, precv, wi_own, wo_own, hin, win, wou, sqs, inv_row, inv_col, nb, prebuf, presend,
+    prerecv, ab, fown, fsend, frecv, csum, csr, hs, hsr,
     kv_s, kv_r, q_s, q_r, d_s, d_r, o_s, o_r, a_s, a_r, wo_s, wo_r, wo_l, p_s, p_r, l_s, own_l,
-    wi_s, wi_r, wu_s, wu_r, sq_s, sq_r, n_s, n_r, nd_s, nd_r, rs_s, rs_r, ag_s, ag_r, ad_s, ad_r,
-    f_s, f_r, c_s, c_r, h_s, h_r,
+    wi_s, wi_r, wu_s, wu_r, sq_s, sq_r, iv_s, iv_r, n_s, n_r, nd_s, nd_r, rs_s, rs_r, ag_s, ag_r,
+    ad_s, ad_r, f_s, f_r, c_s, c_r, h_s, h_r,
 ):
     s = lax.axis_index("seq")
     m = lax.axis_index("mp")
@@ -85,18 +85,38 @@
     drow[0] = doc_here
     qrow[0] = doc_here
     pl.semaphore_wait(barrier, len(friends))
+    for cp in loads:
+        cp.wait()
 
     doc_in = []
     for r in (1, 2, 3):
         doc_in.append(go(remote(drow.at[0], drow.at[r], d_s.at[r], d_r.at[r], dev(dy=r))))
     for r in (1, 2):
         doc_in.append(go(remote(drow.at[0], qrow.at[r], d_s.at[3 + r], d_r.at[3 + r], dev(dz=-r))))
+
+    def direct(h):
+        return [
+            remote(buf.at[0, h], buf.at[r, h], kv_s.at[j, r, h], kv_r.at[j, r, h], dev(dy=r))
+            for r in (1, 3) for j, buf in enumerate((kb, vb))
+        ]
+
+    def relay(h):
+        return [
+            remote(kb.at[1, h], kb.at[2, h], kv_s.at[0, 2, h], kv_r.at[0, 2, h], dev(dy=1)),
+            remote(vb.at[3, h], vb.at[2, h], kv_s.at[1, 2, h], kv_r.at[1, 2, h], dev(dy=3)),
+        ]
+
+    def ask(h):
+        return [
+            remote(qb.at[0, h], qb.at[r, h], q_s.at[r, h], q_r.at[r, h], dev(dz=-r)) for r in (1, 2)
+        ]
+
+    for h in (0, 1):
+        for cp in direct(h):
+            cp.start()
     for h in range(HEADS):
-        for r in ORDER:
-            go(remote(lane(k_ref, h), kb.at[r, h], kv_s.at[0, r, h], kv_r.at[0, r, h], dev(dy=r)))
-            go(remote(lane(v_ref, h), vb.at[r, h], kv_s.at[1, r, h], kv_r.at[1, r, h], dev(dy=r)))
-        for r in (1, 2):
-            go(remote(lane(q_ref, h), qb.at[r, h], q_s.at[r, h], q_r.at[r, h], dev(dz=-r)))
+        for cp in ask(h):
+            cp.start()
 
     wo_loc, wo_rem = [], []
     rows_c = pl.ds(pl.multiple_of(c * WID, 128), WID)
@@ -115,15 +135,20 @@
     live = lax.broadcasted_iota(jnp.int32, (1, SLOTS), 1) < BLOCK * hblk_ref[0]
     want = jnp.where(live, hidx_ref[...], -1)
     pick = (lax.broadcasted_iota(jnp.int32, (NEUR, SLOTS), 0) == want).astype(F32).astype(BF)
-    hin[...] = dot(wi_own[...], pick, ((1,), (0,))).astype(BF)
+    hin[...] = dot(wi_own[...], pick, ((0,), (0,))).astype(BF)
     my_rows = pl.ds(pl.multiple_of(y * SLOTS, 128), SLOTS)
     wou[my_rows, :] = dot(pick, wo_own[...], ((0,), (0,))).astype(BF)
     ct = y // 2
-    win_dst = win.at[rows_c, pl.ds(pl.multiple_of((y % 2) * SLOTS, 128), SLOTS)]
+    left, right = (y + 3) % 4, (y + 1) % 4
+
+    def hot_cols(g):
+        return pl.ds(pl.multiple_of((g % 2) * SLOTS, 128), SLOTS)
+
+    win_dst = win.at[rows_c, hot_cols(y)]
 
     @pl.when(ct == c)
     def _():
-        win[rows_c, pl.ds(pl.multiple_of((y % 2) * SLOTS, 128), SLOTS)] = hin[...]
+        win[rows_c, hot_cols(y)] = hin[...]
 
     wi_peer = remote(hin, win_dst, wi_s.at[0], wi_r.at[y % 2, c], peer)
 
@@ -131,20 +156,26 @@
     def _():
         wi_peer.start()
 
-    wu_in = []
-    for r in ORDER:
-        go(
-            remote(
-                hin, win_dst, wi_s.at[r], wi_r.at[y % 2, c],
-                (z * 4 + (y + r) % 4, 2 * x + ct),
-            )
-        )
-        wu_in.append(
-            go(remote(wou.at[my_rows], wou.at[my_rows], wu_s.at[r], wu_r.at[r], dev(dy=r)))
-        )
-
-    for cp in loads:
-        cp.wait()
+    wi_out = [
+        remote(hin, win_dst, wi_s.at[r], wi_r.at[y % 2, c], (z * 4 + (y + r) % 4, 2 * x + ct))
+        for r in (1, 3)
+    ]
+    wu_out = [
+        remote(wou.at[my_rows], wou.at[my_rows], wu_s.at[r], wu_r.at[r], dev(dy=r)) for r in (1, 3)
+    ]
+
+    def pass_in(j):
+        g = (left, right)[j]
+        part = win.at[j * WID : (j + 1) * WID, hot_cols(g)]
+        return g // 2 == c, remote(
+            part, part, wi_s.at[4 + j], wi_r.at[g % 2, j], dev(dy=(1, 3)[j])
+        )
+
+    def pass_out(j):
+        g = (left, right)[j]
+        part = wou.at[pl.ds(pl.multiple_of(g * SLOTS + j * (SLOTS // 2), 64), SLOTS // 2)]
+        return remote(part, part, wu_s.at[2 * j], wu_r.at[2 * j], dev(dy=(1, 3)[j]))
+
     for cp in doc_in:
         cp.wait_recv()
     for r in range(4):
@@ -186,11 +217,24 @@
         )
 
     def head(h, _):
-        for r in (1, 2):
-            remote(qb.at[0, h], qb.at[r, h], q_s.at[r, h], q_r.at[r, h], dev(dz=-r)).wait_recv()
-        for r in ORDER:
-            remote(kb.at[0, h], kb.at[r, h], kv_s.at[0, r, h], kv_r.at[0, r, h], peer).wait_recv()
-            remote(vb.at[0, h], vb.at[r, h], kv_s.at[1, r, h], kv_r.at[1, r, h], peer).wait_recv()
+        @pl.when(h + 2 < HEADS)
+        def _():
+            for cp in direct(h + 2):
+                cp.start()
+
+        @pl.when(h + 1 < HEADS)
+        def _():
+            pass_on(h + 1)
+
+        @pl.when(h == HEADS - 2)
+        def _():
+            for cp in wi_out + wu_out:
+                cp.start()
+
+        for cp in ask(h):
+            cp.wait_recv()
+        for cp in relay(h):
+            cp.wait_recv()
 
         def away(t, _):
             i = 2 - t
@@ -219,6 +263,13 @@
         st0[h] = both(top, total)
         return 0
 
+    def pass_on(h):
+        for cp in direct(h):
+            cp.wait_recv()
+        for cp in relay(h):
+            cp.start()
+
+    pass_on(0)
     lax.fori_loop(0, HEADS, head, 0)
 
     def swap(h):
@@ -258,6 +309,15 @@
         psend[r] = dot(both_att, wo[(x + r) % 4], ((1,), (0,))).astype(BF)
         p_in.append(go(remote(psend.at[r], precv.at[r], p_s.at[r], p_r.at[r], dev(dx=r))))
     fown[...] = dot(both_att, wo[x], ((1,), (0,))) + res[...].astype(F32)
+
+    for j in (0, 1):
+        here, cp = pass_in(j)
+
+        @pl.when(here)
+        def _():
+            cp.wait_recv()
+            cp.start()
+
     for cp in p_in:
         cp.wait_recv()
     state = (
@@ -266,106 +326,136 @@
     res[...] = state
 
     wide = state.astype(F32)
+    gain = gain_ref[...].astype(F32).reshape(1, WID)
+    nb[0, c] = (wide * gain).astype(BF)
     square = wide * wide
     high = square.astype(BF)
     rest = (square - high.astype(F32)).astype(BF)
     ones = jnp.ones((8, WID), BF)
     sqs[0] = dot(ones, high, ((1,), (1,))) + dot(ones, rest, ((1,), (1,)))
-    sq_in = []
+    n_in, nd_in, iv_in, sq_in = {}, {}, {}, []
+    nd_in[0] = go(remote(nb.at[0, c], nb.at[0, c], nd_s.at[0], nd_r.at[0], peer))
+    for r in ORDER:
+        n_in[r] = go(remote(nb.at[0, c], nb.at[r, c], n_s.at[r], n_r.at[r], dev(dz=r)))
     for j in range(1, 8):
         cp = remote(
             sqs.at[0], sqs.at[j], sq_s.at[j], sq_r.at[j], dev(dx=j // 2, dc=j % 2)
         )
         sq_in.append(go(cp))
-    for cp in sq_in:
+
+    for cp in wu_out:
         cp.wait_recv()
-    squares = sqs[0]
-    for j in range(1, 8):
-        squares = squares + sqs[j]
-    inverse = lax.rsqrt(squares[0:1, :] / D + EPS)
-    column = jnp.transpose(jnp.broadcast_to(inverse, (128, TOK)))
-    column = jnp.concatenate([column] * HEADS, axis=1)
-    gain = gain_ref[...].astype(F32)
-    nb[0, c] = (res[...].astype(F32) * column * gain).astype(BF)
-
-    n_in = {}
-    nd_in = {}
-    nd_in[0] = go(remote(nb.at[0, c], nb.at[0, c], nd_s.at[0], nd_r.at[0], peer))
-    for r in ORDER:
-        n_in[r] = go(remote(nb.at[0, c], nb.at[r, c], n_s.at[r], n_r.at[r], dev(dz=r)))
-
-    for cp in wu_in:
-        cp.wait_recv()
+    for j in (0, 1):
+        go(pass_out(j))
+
     for gi in (0, 1):
         for cs in (0, 1):
-            @pl.when(jnp.logical_not(jnp.logical_and(y == 2 * c + gi, c == cs)))
+            g = 2 * c + gi
+            had = jnp.logical_or(
+                jnp.logical_and(g == y, c == cs), g == (left, right)[cs]
+            )
+
+            @pl.when(jnp.logical_not(had))
             def _():
                 remote(hin, win_dst, wi_s.at[0], wi_r.at[gi, cs], peer).wait_recv()
 
     csum[...] = jnp.zeros_like(csum)
     rs_in, ag_in, ad_in, f_in = {}, {}, {}, {}
-    my64 = pl.ds(pl.multiple_of(x * 64, 64), 64)
-
-    def stage_a(r):
-        if r:
-            n_in[r].wait_recv()
-            nd_in[r] = go(remote(nb.at[r, c], nb.at[r, c], nd_s.at[r], nd_r.at[r], peer))
-
-    def stage_b(r):
-        nd_in[r].wait_recv()
-        rows = jnp.concatenate([nb[r, 0], nb[r, 1]], axis=1)
+    parts = ((0, 0, 128), (1, 0, TOK), (3, 0, TOK), (2, 0, TOK), (0, 128, 128))
+
+    def quarter(b, at):
+        _, first, n = parts[b]
+        return pl.ds(pl.multiple_of(first + at * (n // 4), 32), n // 4)
+
+    def columns_of(r, row):
+        inv_col[r] = jnp.transpose(jnp.broadcast_to(row, (128, TOK)))
+
+    def stage_n(b):
+        for cp in sq_in:
+            cp.wait_recv()
+        squares = sqs[0]
+        for j in range(1, 8):
+            squares = squares + sqs[j]
+        inv_row[0] = lax.rsqrt(squares / D + EPS)
+        for r in ORDER:
+            iv_in[r] = go(
+                remote(inv_row.at[0], inv_row.at[r], iv_s.at[r], iv_r.at[r], dev(dz=r))
+            )
+        columns_of(0, inv_row[0][0:1, :])
+
+    def stage_a(b):
+        r = parts[b][0]
+        n_in[r].wait_recv()
+        nd_in[r] = go(remote(nb.at[r, c], nb.at[r, c], nd_s.at[r], nd_r.at[r], peer))
+
+    def stage_b(b):
+        r, first, n = parts[b]
+        if b < 4:
+            nd_in[r].wait_recv()
+        at = slice(first, first + n)
+        rows = jnp.concatenate([nb[r, 0, at], nb[r, 1, at]], axis=1)
         pre = dot(rows, win[...], ((1,), (0,)))
-        prebuf[r] = pre
-        presend[r] = pre.astype(BF)
+        prebuf[r, at] = pre
+        presend[r, at] = pre.astype(BF)
         for e in (2, 1, 3):
-            there = pl.ds(pl.multiple_of(((x + e) % 4) * 64, 64), 64)
-            rs_in[r, e] = go(
+            rs_in[b, e] = go(
                 remote(
-                    presend.at[r, there], prerecv.at[r, e], rs_s.at[r, e], rs_r.at[r, e],
-                    dev(dx=e),
+                    presend.at[r, quarter(b, (x + e) % 4)], prerecv.at[b, e, 0 : n // 4],
+                    rs_s.at[b, e], rs_r.at[b, e], dev(dx=e),
                 )
             )
 
-    def stage_c(r):
+    def stage_c(b):
+        r, first, n = parts[b]
         for e in (1, 3, 2):
-            rs_in[r, e].wait_recv()
+            rs_in[b, e].wait_recv()
+        if r:
+            iv_in[r].wait_recv()
+            columns_of(r, inv_row[r][0:1, :])
+        here = quarter(b, x)
+        q = slice(0, n // 4)
         pre = (
-            prebuf[r, my64, :] + prerecv[r, 1].astype(F32) + prerecv[r, 2].astype(F32)
-            + prerecv[r, 3].astype(F32)
-        )
-        active = jnp.maximum(pre, 0.0)
+            prebuf[r, here, :] + prerecv[b, 1, q].astype(F32) + prerecv[b, 2, q].astype(F32)
+            + prerecv[b, 3, q].astype(F32)
+        )
+        factor = inv_col[r, here, :]
+        active = jnp.maximum(pre, 0.0) * jnp.concatenate([factor] * 6, axis=1)
         csum[...] += jnp.sum(active, axis=0, keepdims=True)
-        ab[r, c, my64, :] = active.astype(BF)
+        ab[r, c, here, :] = active.astype(BF)
         for e in (2, 1, 3):
-            ag_in[r, e] = go(
+            ag_in[b, e] = go(
                 remote(
-                    ab.at[r, c, my64], ab.at[r, c, my64], ag_s.at[r, e], ag_r.at[r, e], dev(dx=e)
+                    ab.at[r, c, here], ab.at[r, c, here], ag_s.at[b, e], ag_r.at[b, e], dev(dx=e)
                 )
             )
 
-    def stage_d(r):
+    def stage_d(b):
+        r, first, n = parts[b]
         for e in (1, 3, 2):
-            ag_in[r, e].wait_recv()
-        ad_in[r] = go(remote(ab.at[r, c], ab.at[r, c], ad_s.at[r], ad_r.at[r], peer))
-
-    def stage_e(r):
-        ad_in[r].wait_recv()
-        rows = jnp.concatenate([ab[r, 0], ab[r, 1]], axis=1)
+            ag_in[b, e].wait_recv()
+        block = ab.at[r, c, first : first + n]
+        ad_in[b] = go(remote(block, block, ad_s.at[b], ad_r.at[b], peer))
+
+    def stage_e(b):
+        r, first, n = parts[b]
+        if b == 0:
+            wu_relayed = (pass_out(0), pass_out(1))
+            for cp in wu_relayed:
+                cp.wait_recv()
+        ad_in[b].wait_recv()
+        at = slice(first, first + n)
+        rows = jnp.concatenate([ab[r, 0, at], ab[r, 1, at]], axis=1)
         part = dot(rows, wou[...], ((1,), (0,)))
         if r == 0:
-            fown[...] = part
+            fown[at] = part + res[at].astype(F32)
         else:
             fsend[r] = part.astype(BF)
             f_in[r] = go(remote(fsend.at[r], frecv.at[r], f_s.at[r], f_r.at[r], dev(dz=-r)))
 
-    plan = (
-        (stage_a, 0), (stage_b, 0), (stage_a, 1), (stage_b, 1), (stage_c, 0), (stage_a, 3),
-        (stage_b, 3), (stage_c, 1), (stage_d, 0), (stage_a, 2), (stage_b, 2), (stage_c, 3),
-        (stage_d, 1), (stage_e, 0), (stage_c, 2), (stage_d, 3), (stage_e, 1), (stage_d, 2),
-        (stage_e, 3), (stage_e, 2),
-    )
-    for stage, r in plan:
-        stage(r)
+    stage = {"n": stage_n, "a": stage_a, "b": stage_b, "c": stage_c, "d": stage_d, "e": stage_e}
+    plan = "b0 n0 c0 a1 b1 d0 a2 b2 c1 e0 a3 b3 c2 d1 b4 c3 d2 e1 c4 d3 e2 d4 e3"
+    for word in plan.split():
+        stage[word[0]](int(word[1]))
 
     c_in = []
     for r in (1, 2, 3):
@@ -393,11 +483,11 @@
             def _():
                 hsr[y] = hs[gi]
 
+    stage_e(4)
     for r in ORDER:
         f_in[r].wait_recv()
     out_ref[...] = (
-        res[...].astype(F32) + fown[...] + frecv[1].astype(F32) + frecv[2].astype(F32)
-        + frecv[3].astype(F32)
+        fown[...] + frecv[1].astype(F32) + frecv[2].astype(F32) + frecv[3].astype(F32)
     ).astype(BF)
 
     for src in range(4):
@@ -418,7 +508,18 @@
     def _():
         wi_peer.wait_send()
 
+    for cp in wi_out + wu_out:
+        cp.wait_send()
+    for j in (0, 1):
+        here, cp = pass_in(j)
+
+        @pl.when(here)
+        def _():
+            cp.wait_send()
+
     def drain(h, _):
+        for cp in direct(h) + relay(h) + ask(h):
+            cp.wait_send()
         for i in (1, 2):
             for cp in back(i, h):
                 cp.wait_send()
@@ -443,19 +544,20 @@
         V((2, HEADS, 128, TOK), BF), V((2, HEADS, 8, TOK), F32),
         V((2, HEADS, TOK, 128), BF), V((4, 2 * WID, WID), BF), V((TOK, WID), BF),
         V((4, TOK, WID), BF), V((4, TOK, WID), BF),
-        V((WID, NEUR), BF), V((NEUR, WID), BF), V((WID, SLOTS), BF),
+        V((NEUR, WID), BF), V((NEUR, WID), BF), V((WID, SLOTS), BF),
         V((2 * WID, 2 * SLOTS), BF), V((4 * SLOTS, WID), BF),
-        V((8, 8, TOK), F32), V((4, 2, TOK, WID), BF), V((4, TOK, 2 * SLOTS), F32),
-        V((4, TOK, 2 * SLOTS), BF), V((4, 4, 64, 2 * SLOTS), BF), V((4, 2, TOK, 2 * SLOTS), BF),
+        V((8, 8, TOK), F32), V((4, 8, TOK), F32), V((4, TOK, 128), F32), V((4, 2, TOK, WID), BF),
+        V((4, TOK, 2 * SLOTS), F32),
+        V((4, TOK, 2 * SLOTS), BF), V((5, 4, 64, 2 * SLOTS), BF), V((4, 2, TOK, 2 * SLOTS), BF),
         V((TOK, WID), F32), V((4, TOK, WID), BF), V((4, TOK, WID), BF),
         V((8, 2 * SLOTS), F32), V((4, 8, 2 * SLOTS), F32), V((2, 8, SLOTS), F32),
         V((4, 8, SLOTS), F32),
         dma((2, 4, HEADS)), dma((2, 4, HEADS)), dma((3, HEADS)), dma((3, HEADS)),
         dma((6,)), dma((6,)), dma((2, 2, HEADS)), dma((2, 2, HEADS)),
         dma((HEADS,)), dma((HEADS,)), dma((4,)), dma((4,)), dma((4,)), dma((4,)), dma((4,)),
-        dma((3,)), dma((3, HEADS)), dma((4,)), dma((2, 2)), dma((4,)), dma((4,)),
-        dma((8,)), dma((8,)), dma((4,)), dma((4,)), dma((4,)), dma((4,)),
-        dma((4, 4)), dma((4, 4)), dma((4, 4)), dma((4, 4)), dma((4,)), dma((4,)),
+        dma((3,)), dma((3, HEADS)), dma((6,)), dma((2, 2)), dma((4,)), dma((4,)),
+        dma((8,)), dma((8,)), dma((4,)), dma((4,)), dma((4,)), dma((4,)), dma((4,)), dma((4,)),
+        dma((5, 4)), dma((5, 4)), dma((5, 4)), dma((5, 4)), dma((5,)), dma((5,)),
         dma((4,)), dma((4,)), dma((4,)), dma((4,)), dma((2, 2)), dma((4,)),
     ]
     return pl.pallas_call(
@@ -472,7 +574,7 @@
         name="layer",
     )(
         queries, keys, values, resid, doc_ids.reshape(1, TOK), out_proj,
-        ffn_gain.reshape(1, WID), w_in, w_out, hot_index, hot_blocks,
+        ffn_gain, w_in.T, w_out, hot_index, hot_blocks,
     )
 
 

time: 147 us -> 136 us (0.925)
  the two profiles are of different devices: /device:TPU:1 before, /device:TPU:15 now
where the time goes in v2:
time: 136 us; the launch traced here: 135 us
  Pallas kernels  131 us (96%)
  local copies, waits for them, and re-layouts  2.97 us (2%)
    pallas_call x1, Pallas kernels, local(): pl.pallas_call(kernel, out_shape=(jax.ShapeDtypeStruct((TOK, WID), BF), j...  131 us
    unnamed x2, local copies, waits for them, and re-layouts  2.97 us

profile of v2, /device:TPU:15, one launch (start us, length us, event | category | flops | bytes accessed | tf_op | source)
XLA Modules:
  0.0 135.4 jit_solution(15599351716648717187)
XLA Ops:
  1.3 131.1 %layer.1 = (bf16[256,640]{1,0:T(8,128)(2,1)}, f32[1,384]{1,0:T(1,128)}) custom-call(bf16[256,640]{1,0:T(8,128)(2,1)} %q_ref.1, bf16[256,640]{1,0:T(8,128)(2,1)} %k_ref.1, bf16[256,640]{1,0:T(8,128)(2,1)} %v_ref.1, bf16[256,640]{1,0:T(8,128)(2,1)} %resid_ref.1, s32[1,256]{1,0:T(1,128)} %bitcast.3, bf16[640,5120]{1,0:T(8,128)(2,1)} %oproj_ref.1, ...), custom_call_target="tpu_custom_call" | custom-call | tf_op jit(solution)/shard_map/layer/pallas_call | solution.py:563
  132.4 1.7 %copy.16 = bf16[256,640]{1,0:T(8,128)(2,1)} copy(bf16[256,640]{1,0:T(8,128)(2,1)} %get-tuple-element.4) | data formatting | bytes 655360
  134.1 1.2 copy.17

commit v3 on v2

v3 whole, which is shorter than its diff:
```python
import jax
import jax.numpy as jnp
from jax import lax
from jax.experimental import pallas as pl
from jax.experimental.pallas import tpu as pltpu
from jax.sharding import PartitionSpec as P

HEAD_DIM = 128
HEADS = 5
TOK = 256
WID = 640
SLOTS = 384
BLOCK = 128
NEUR = 864
D = 5120
TOKENS = 4096
EPS = 1e-05
LOW = -1e9
MASKED = -2e9
SCALE2 = HEAD_DIM ** (-0.5) * 1.4426950408889634
BF = jnp.bfloat16
F32 = jnp.float32
ORDER = (1, 3, 2)
PLAN = (
    "t4", "b0", "s0", "t5", "t6", "r0", "t3", "a2", "b1", "a7", "n0", "c0", "b2", "b7", "r1",
    "a4", "d0", "b4", "r2", "r7", "a5", "c1", "g0", "w0", "b5", "a3", "a6", "c2", "c4", "c7",
    "b3", "d1", "r5", "b6", "d2", "g4", "d7", "r3", "e4", "g1", "c5", "r6", "e0", "e1", "g2",
    "g7", "c3", "e2", "d5", "c6", "h0", "e7", "d3", "g5", "d6", "e5", "g3", "g6", "e3", "e6",
)


def dot(a, b, dims):
    return lax.dot_general(a, b, (dims, ((), ())), preferred_element_type=F32)


def kernel(
    q_ref, k_ref, v_ref, resid_ref, doc_ref, oproj_ref, gain_ref, win_ref, wout_ref, hidx_ref,
    hblk_ref, out_ref, hm_ref,
    qb, kvb, drow, qrow, kcol, acc0, st0, osend, ssend, orecv, srecv, att, wo, res,
    psend, precv, prel, pnear, wi_own, wo_own, hin, win, wou, sqs, inv_row, inv_col, nb, prebuf,
    presend, prerecv, relrecv, relsend, ab, fown, fsend, frecv, csum, csr, hs, hsr,
    out_s, kv_r, q_r, o_r, p_r, l_s, own_l, wi_s, wi_r, n_r, nd_r, rel_r, rs_r, ag_r, fwd_r, ad_r,
    one_r, h_s, h_r,
):
    s = lax.axis_index("seq")
    m = lax.axis_index("mp")
    z, y, x, c = s // 4, s % 4, m // 2, m % 2

    def dev(dz=0, dy=0, dx=0, dc=0):
        return (((z + dz) % 4) * 4 + (y + dy) % 4, ((x + dx) % 4) * 2 + (c + dc) % 2)

    def remote(src, dst, ss, rs, device):
        return pltpu.make_async_remote_copy(
            src_ref=src, dst_ref=dst, send_sem=ss, recv_sem=rs, device_id=device,
            device_id_type=pl.DeviceIdType.MESH,
        )

    peer = dev(dc=1)

    def go(cp):
        cp.start()
        return cp

    def arrived(ref, sem):
        remote(ref, ref, sem, sem, peer).wait_recv()

    def gone(ref, sem):
        remote(ref, ref, sem, sem, peer).wait_send()

    (S_KV, S_Q, S_DK, S_DQ, S_O, S_A, S_WO, S_P, S_WU, S_SQ, S_IV, S_N, S_ND, S_X, S_AD, S_F,
     S_C) = [out_s.at[i] for i in range(17)]
    R_DK, R_DQ, R_A, R_WO, R_WU, R_WP, R_SQ, R_IV, R_F, R_C, R_WL = [
        one_r.at[i] for i in range(11)
    ]

    def lane(ref, h):
        return ref.at[:, h * HEAD_DIM : (h + 1) * HEAD_DIM]

    for h in range(HEADS):
        pltpu.make_async_copy(lane(k_ref, h), kvb.at[0, h, 0], own_l.at[0]).start()
        pltpu.make_async_copy(lane(v_ref, h), kvb.at[0, h, 1], own_l.at[0]).start()
        pltpu.make_async_copy(lane(q_ref, h), qb.at[0, h], own_l.at[1]).start()
    big = [
        pltpu.make_async_copy(win_ref, wi_own, l_s.at[0]),
        pltpu.make_async_copy(wout_ref, wo_own, l_s.at[1]),
        pltpu.make_async_copy(resid_ref, res, l_s.at[2]),
    ]
    for cp in big:
        cp.start()

    barrier = pltpu.get_barrier_semaphore()
    friends = [peer]
    for r in (1, 2, 3):
        friends += [dev(dy=r), dev(dy=r, dc=1), dev(dz=r), dev(dx=r), dev(dx=r, dc=1)]
    for f in friends:
        pl.semaphore_signal(barrier, inc=1, device_id=f, device_id_type=pl.DeviceIdType.MESH)
    doc_here = jnp.broadcast_to(doc_ref[...].astype(F32), (8, TOK))
    drow[0] = doc_here
    qrow[0] = doc_here
    pl.semaphore_wait(barrier, len(friends))
    for r in (1, 2, 3):
        go(remote(drow.at[0], drow.at[r], S_DK, R_DK, dev(dy=r)))
    for r in (1, 2):
        go(remote(drow.at[0], qrow.at[r], S_DQ, R_DQ, dev(dz=-r)))
    pltpu.make_async_copy(kvb.at[0], kvb.at[0], own_l.at[0]).wait()
    pltpu.make_async_copy(qb.at[0], qb.at[0], own_l.at[1]).wait()

    def direct(h):
        return [
            remote(kvb.at[0, h], kvb.at[r, h], S_KV, kv_r.at[r // 2, h], dev(dy=r)) for r in (1, 3)
        ]

    def relay(h):
        return [
            remote(kvb.at[1, h, 0], kvb.at[2, h, 0], S_KV, kv_r.at[2, h], dev(dy=1)),
            remote(kvb.at[3, h, 1], kvb.at[2, h, 1], S_KV, kv_r.at[2, h], dev(dy=3)),
        ]

    def ask(h):
        return [remote(qb.at[0, h], qb.at[r, h], S_Q, q_r.at[h], dev(dz=-r)) for r in (1, 2)]

    for h in range(HEADS):
        if h < 2:
            for cp in direct(h):
                cp.start()
        for cp in ask(h):
            cp.start()

    rows_c = pl.ds(pl.multiple_of(c * WID, 128), WID)

    def chunk(of):
        return oproj_ref.at[:, pl.ds(pl.multiple_of(of * WID, 128), WID)]

    rows_o = pl.ds(pl.multiple_of((1 - c) * WID, 128), WID)
    wo_loc = [
        pltpu.make_async_copy(chunk(2 * d + c), wo.at[d, rows_c, :], R_WL) for d in range(4)
    ]
    wo_rem = [
        remote(chunk(2 * d + 1 - c), wo.at[d, rows_c, :], S_WO, R_WO, peer) for d in range(4)
    ]

    ct = y // 2
    left, right = (y + 3) % 4, (y + 1) % 4

    def hot_cols(g):
        return pl.ds(pl.multiple_of((g % 2) * SLOTS, 128), SLOTS)

    win_dst = win.at[rows_c, hot_cols(y)]
    my_rows = pl.ds(pl.multiple_of(y * SLOTS, 128), SLOTS)
    wi_peer = remote(hin, win_dst, wi_s.at[0], wi_r.at[y % 2, c], peer)

    def choose():
        for cp in big:
            cp.wait()
        live = lax.broadcasted_iota(jnp.int32, (1, SLOTS), 1) < BLOCK * hblk_ref[0]
        want = jnp.where(live, hidx_ref[...], -1)
        pick = (lax.broadcasted_iota(jnp.int32, (NEUR, SLOTS), 0) == want).astype(F32).astype(BF)
        hin[...] = dot(wi_own[...], pick, ((0,), (0,))).astype(BF)
        wou[my_rows, :] = dot(pick, wo_own[...], ((0,), (0,))).astype(BF)

        @pl.when(ct == c)
        def _():
            win[rows_c, hot_cols(y)] = hin[...]

        @pl.when(ct != c)
        def _():
            wi_peer.start()

    wi_out = [
        remote(hin, win_dst, wi_s.at[r], wi_r.at[y % 2, c], (z * 4 + (y + r) % 4, 2 * x + ct))
        for r in (1, 3)
    ]
    wu_out = [
        remote(wou.at[my_rows], wou.at[my_rows], S_WU, R_WU, dev(dy=r)) for r in (1, 3)
    ]

    def pass_in(j):
        g = (left, right)[j]
        part = win.at[j * WID : (j + 1) * WID, hot_cols(g)]
        return g // 2 == c, remote(
            part, part, wi_s.at[4 + j], wi_r.at[g % 2, j], dev(dy=(1, 3)[j])
        )

    def pass_out(j):
        g = (left, right)[j]
        part = wou.at[pl.ds(pl.multiple_of(g * SLOTS + j * (SLOTS // 2), 64), SLOTS // 2)]
        return remote(part, part, S_WU, R_WP, dev(dy=(1, 3)[j]))

    choose()
    arrived(drow.at[1:4], R_DK)
    arrived(qrow.at[1:3], R_DQ)
    for r in range(4):
        kcol[r] = jnp.transpose(jnp.broadcast_to(drow[r][0:1, :], (128, TOK)))

    def pair(h, i, r, qd, causal=False):
        sc = dot(kvb[r, h, 0], qb[i, h], ((1,), (1,)))
        kd = kcol[r]
        mask = jnp.concatenate([kd, kd], axis=1) == qd
        if causal:
            key_at = lax.broadcasted_iota(jnp.int32, (TOK, TOK), 0)
            query_at = lax.broadcasted_iota(jnp.int32, (TOK, TOK), 1)
            mask = mask & (key_at <= query_at)
        sc = jnp.where(mask, sc, MASKED)
        top = jnp.maximum(jnp.max(sc, axis=0, keepdims=True), LOW)
        p = jnp.exp2((sc - top) * SCALE2)
        total = jnp.sum(p, axis=0, keepdims=True)
        return top, total, dot(kvb[r, h, 1], p.astype(BF), ((0,), (0,)))

    def together(results):
        top = results[0][0]
        for other, _, _ in results[1:]:
            top = jnp.maximum(top, other)
        total, acc = 0.0, 0.0
        for own, part, mixed in results:
            factor = jnp.exp2((own - top) * SCALE2)
            total = total + part * factor
            acc = acc + mixed * factor
        return top, total, acc

    def both(top, total):
        row = lax.broadcasted_iota(jnp.int32, (8, TOK), 0)
        return jnp.where(row == 0, top, total)

    def back(i, h):
        return (
            remote(
                osend.at[i - 1, h, 0:128], orecv.at[i - 1, h, 0:128], S_O, o_r.at[h],
                (((z + i) % 4) * 4 + y, m),
            ),
            remote(
                ssend.at[i - 1, h], srecv.at[i - 1, h], S_O, o_r.at[h],
                (((z + i) % 4) * 4 + y, m),
            ),
        )

    def head(h, _):
        @pl.when(h + 2 < HEADS)
        def _():
            for cp in direct(h + 2):
                cp.start()

        arrived(qb.at[1:3, h], q_r.at[h])
        q0 = qrow[0][0:1, :]
        q1 = jnp.where(z + 1 <= 3, qrow[1][0:1, :], -5.0)
        q2 = jnp.where(z + 2 <= 3, qrow[2][0:1, :], -5.0)

        def shared(n):
            if n == 0:
                return pair(h, 0, 0, q0, True)
            own = n <= y
            slot = jnp.where(own, n, jnp.where(n == y + 1, 0, n - 1))
            return pair(h, jnp.where(own, 0, 2), slot, jnp.where(own, q0, q2))

        near, mix = {}, {}
        for n in (0, 1, 3):
            near[n] = pair(h, 1, n, q1)
        for n in (0, 1, 4):
            mix[n] = shared(n)

        @pl.when(h + 1 < HEADS)
        def _():
            pass_on(h + 1)

        @pl.when(h == HEADS - 2)
        def _():
            for cp in wi_out:
                cp.start()

        arrived(kvb.at[2, h], kv_r.at[2, h])
        for n in (2, 3):
            mix[n] = shared(n)
        far = [
            (jnp.where(n <= y, LOW, mix[n][0]), mix[n][1], mix[n][2]) for n in (1, 2, 3)
        ] + [mix[4]]
        for i, parts_of in ((2, far), (1, None)):
            if i == 1:
                near[2] = pair(h, 1, 2, q1)
                parts_of = [near[n] for n in range(4)]
            top, total, acc = together(parts_of)
            osend[i - 1, h, 0:128] = acc.astype(BF)
            ssend[i - 1, h] = both(top, total)
            for cp in back(i, h):
                cp.start()
        top, total, acc = together(
            [mix[0]] + [(jnp.where(n <= y, mix[n][0], LOW), mix[n][1], mix[n][2]) for n in (1, 2, 3)]
        )
        acc0[h] = acc
        st0[h] = both(top, total)

        @pl.when(h == 0)
        def _():
            for cp in wo_loc + wo_rem:
                cp.start()

        return 0

    def pass_on(h):
        for cp in direct(h):
            cp.wait_recv()
        for cp in relay(h):
            cp.start()

    pass_on(0)
    lax.fori_loop(0, HEADS, head, 0)

    def swap(h):
        return remote(att.at[c, h], att.at[c, h], S_A, R_A, peer)

    def merge(h, _):
        arrived(orecv.at[:, h], o_r.at[h])
        t0, t1, t2 = st0[h][0:1, :], srecv[0, h][0:1, :], srecv[1, h][0:1, :]
        n0, n1, n2 = st0[h][1:2, :], srecv[0, h][1:2, :], srecv[1, h][1:2, :]
        top = jnp.maximum(t0, jnp.maximum(t1, t2))
        f0 = jnp.exp2((t0 - top) * SCALE2)
        f1 = jnp.exp2((t1 - top) * SCALE2)
        f2 = jnp.exp2((t2 - top) * SCALE2)
        inv = 1.0 / (n0 * f0 + n1 * f1 + n2 * f2)
        mixed = (
            acc0[h] * (f0 * inv)
            + orecv[0, h, 0:128].astype(F32) * (f1 * inv)
            + orecv[1, h, 0:128].astype(F32) * (f2 * inv)
        )
        att[c, h] = jnp.transpose(mixed).astype(BF)
        swap(h).start()
        return 0

    lax.fori_loop(0, HEADS, merge, 0)

    pltpu.make_async_copy(wo.at[:, rows_c, :], wo.at[:, rows_c, :], R_WL).wait()
    arrived(wo.at[:, rows_o, :], R_WO)
    arrived(att.at[1 - c], R_A)
    both_att = jnp.concatenate([att[i, h] for i in (0, 1) for h in range(HEADS)], axis=1)

    def span(k, j):
        return slice(128 * k + 64 * j, 128 * k + 64 * j + 64)

    def project(dx, k):
        return dot(both_att[128 * k : 128 * k + 128], wo[(x + dx) % 4], ((1,), (0,)))

    def across(k):
        psend[2, 128 * k : 128 * k + 128] = project(2, k).astype(BF)
        for j, e in ((0, 1), (1, 3)):
            go(remote(psend.at[2, span(k, j)], prel.at[k, j], S_P, p_r.at[k], dev(dx=e)))

    def beside(k):
        for j, e in ((0, 1), (1, 3)):
            pnear[j, 128 * k : 128 * k + 128] = project(e, k)
            rows = span(k, 1 - j)
            psend[e, rows] = pnear[j, rows].astype(BF)
            half = slice(64 - 64 * j, 128 - 64 * j)
            go(remote(psend.at[e, rows], precv.at[k, j, half], S_P, p_r.at[2 + k], dev(dx=e)))

    def onward(k):
        arrived(prel.at[k], p_r.at[k])
        for j, e in ((0, 1), (1, 3)):
            rows = span(k, j)
            psend[e, rows] = (pnear[j, rows] + prel[k, j].astype(F32)).astype(BF)
            half = slice(64 * j, 64 * j + 64)
            go(remote(psend.at[e, rows], precv.at[k, j, half], S_P, p_r.at[2 + k], dev(dx=e)))

    across(0)
    beside(0)
    across(1)

    for j in (0, 1):
        here, cp = pass_in(j)

        @pl.when(here)
        def _():
            cp.wait_recv()
            cp.start()

    for cp in wu_out:
        cp.start()

    onward(0)
    beside(1)
    for k in (0, 1):
        at = slice(128 * k, 128 * k + 128)
        fown[at] = project(0, k) + res[at].astype(F32)
    onward(1)

    n_in, nd_in = {}, {}

    def tokens(r, k):
        half = slice(128 * k, 128 * k + 128)
        n_in[r, k] = go(
            remote(nb.at[0, c, half], nb.at[r, c, half], S_N, n_r.at[r - 1, k], dev(dz=r))
        )

    def mate(r, k):
        half = nb.at[r, c, 128 * k : 128 * k + 128]
        nd_in[r, k] = go(remote(half, half, S_ND, nd_r.at[r, k], peer))

    gain = gain_ref[...].astype(F32).reshape(1, WID)

    def settle(k):
        at = slice(128 * k, 128 * k + 128)
        arrived(precv.at[k], p_r.at[2 + k])
        state = (fown[at] + precv[k, 0].astype(F32) + precv[k, 1].astype(F32)).astype(BF)
        res[at] = state
        nb[0, c, at] = (state.astype(F32) * gain).astype(BF)
        mate(0, k)

    settle(0)
    for r in (1, 3):
        tokens(r, 0)

    def stage_w(b):
        arrived(wou.at[0 : 2 * SLOTS], R_WU)
        for j in (0, 1):
            go(pass_out(j))

    for gi in (0, 1):
        for cs in (0, 1):
            g = 2 * c + gi
            had = jnp.logical_or(
                jnp.logical_and(g == y, c == cs), g == (left, right)[cs]
            )

            @pl.when(jnp.logical_not(had))
            def _():
                remote(hin, win_dst, wi_s.at[0], wi_r.at[gi, cs], peer).wait_recv()

    csum[...] = jnp.zeros_like(csum)
    parts = tuple(
        (r, 128 * k, 128)
        for r, k in ((0, 0), (0, 1), (1, 0), (3, 1), (2, 0), (2, 1), (1, 1), (3, 0))
    )

    plain = (4,)

    def quarter(b, at):
        _, first, n = parts[b]
        return pl.ds(pl.multiple_of(first + at * (n // 4), 32), n // 4)

    def eighth(b, at, j):
        _, first, n = parts[b]
        return pl.ds(pl.multiple_of(first + at * (n // 4) + j * (n // 8), 16), n // 8)

    def columns_of(r, row):
        inv_col[r] = jnp.transpose(jnp.broadcast_to(row, (128, TOK)))

    def stage_n(b):
        arrived(sqs.at[1:8], R_SQ)
        squares = sqs[0]
        for j in range(1, 8):
            squares = squares + sqs[j]
        inv_row[0] = lax.rsqrt(squares / D + EPS)
        for r in ORDER:
            go(remote(inv_row.at[0], inv_row.at[r], S_IV, R_IV, dev(dz=r)))
        columns_of(0, inv_row[0][0:1, :])

    def stage_a(b):
        r, first, _ = parts[b]
        if r:
            n_in[r, first // 128].wait_recv()
            mate(r, first // 128)

    def stage_b(b):
        r, first, n = parts[b]
        nd_in[r, first // 128].wait_recv()
        at = slice(first, first + n)
        rows = jnp.concatenate([nb[r, 0, at], nb[r, 1, at]], axis=1)
        pre = dot(rows, win[...], ((1,), (0,)))
        prebuf[r, at] = pre
        presend[r, at] = pre.astype(BF)
        h = n // 8
        if b in plain:
            for e in (2, 1, 3):
                go(
                    remote(
                        presend.at[r, quarter(b, (x + e) % 4)], prerecv.at[b, e - 1], S_X,
                        rs_r.at[b], dev(dx=e),
                    )
                )
            return
        for j, e in ((0, 1), (1, 3)):
            rest = slice(h - j * h, 2 * h - j * h)
            go(
                remote(
                    presend.at[r, eighth(b, (x + 2) % 4, j)], relrecv.at[b, j], S_X, rel_r.at[b],
                    dev(dx=e),
                )
            )
            go(
                remote(
                    presend.at[r, eighth(b, (x + e) % 4, 1 - j)], prerecv.at[b, j, rest], S_X,
                    rs_r.at[b], dev(dx=e),
                )
            )

    def stage_r(b):
        r, first, n = parts[b]
        h = n // 8
        arrived(relrecv.at[b], rel_r.at[b])
        for j, e in ((0, 1), (1, 3)):
            half = slice(j * h, j * h + h)
            there = eighth(b, (x + e) % 4, j)
            relsend[b, j] = (
                prebuf[r, there, :] + relrecv[b, j].astype(F32)
            ).astype(BF)
            go(remote(relsend.at[b, j], prerecv.at[b, j, half], S_X, rs_r.at[b], dev(dx=e)))

    def stage_c(b):
        r, first, n = parts[b]
        arrived(prerecv.at[b, 0 : 3 if b in plain else 2], rs_r.at[b])
        if b == 2:
            arrived(inv_row.at[1:4], R_IV)
        if r and first == 0:
            columns_of(r, inv_row[r][0:1, :])
        here = quarter(b, x)
        q = slice(0, n // 4)
        pre = (
            prebuf[r, here, :] + prerecv[b, 0, q].astype(F32) + prerecv[b, 1, q].astype(F32)
        )
        if b in plain:
            pre = pre + prerecv[b, 2].astype(F32)
        factor = inv_col[r, here, :]
        active = jnp.maximum(pre, 0.0) * jnp.concatenate([factor] * 6, axis=1)
        csum[...] += jnp.sum(active, axis=0, keepdims=True)
        ab[r, c, here, :] = active.astype(BF)
        for e in (2, 1, 3) if b in plain else (1, 3):
            go(remote(ab.at[r, c, here], ab.at[r, c, here], S_X, ag_r.at[b], dev(dx=e)))

    def stage_d(b):
        r, first, n = parts[b]
        arrived(ab.at[r, c, first : first + n // 2], ag_r.at[b])
        for j, e in ((0, 1), (1, 3)):
            block = ab.at[r, c, eighth(b, (x - e) % 4, j)]
            go(remote(block, block, S_X, fwd_r.at[b], dev(dx=e)))

    def stage_g(b):
        r, first, n = parts[b]
        if b in plain:
            arrived(ab.at[r, c, first : first + 3 * n // 4], ag_r.at[b])
        else:
            arrived(ab.at[r, c, first : first + n // 4], fwd_r.at[b])
        block = ab.at[r, c, first : first + n]
        go(remote(block, block, S_AD, ad_r.at[b], peer))

    def stage_e(b):
        r, first, n = parts[b]
        if b == 4:
            arrived(wou.at[0:SLOTS], R_WP)
        arrived(ab.at[r, 1 - c, first : first + n], ad_r.at[b])
        at = slice(first, first + n)
        rows = jnp.concatenate([ab[r, 0, at], ab[r, 1, at]], axis=1)
        part = dot(rows, wou[...], ((1,), (0,)))
        if r == 0:
            fown[at] = part + res[at].astype(F32)
        else:
            fsend[r, at] = part.astype(BF)
            go(remote(fsend.at[r, at], frecv.at[r, at], S_F, R_F, dev(dz=-r)))

    def stage_s(b):
        settle(1)
        wide = res[...].astype(F32)
        square = wide * wide
        high = square.astype(BF)
        rest = (square - high.astype(F32)).astype(BF)
        ones = jnp.ones((8, WID), BF)
        sqs[0] = dot(ones, high, ((1,), (1,))) + dot(ones, rest, ((1,), (1,)))
        for j in range(1, 8):
            go(remote(sqs.at[0], sqs.at[j], S_SQ, R_SQ, dev(dx=j // 2, dc=j % 2)))

    def stage_t(b):
        tokens(parts[b][0], parts[b][1] // 128)

    def stage_h(b):
        for r in (1, 2, 3):
            go(remote(csum, csr.at[r], S_C, R_C, dev(dx=r)))

    stage = {
        "n": stage_n, "a": stage_a, "b": stage_b, "r": stage_r, "c": stage_c, "d": stage_d,
        "g": stage_g, "e": stage_e, "h": stage_h, "s": stage_s, "t": stage_t, "w": stage_w,
    }
    for word in PLAN:
        stage[word[0]](int(word[1]))

    arrived(csr.at[1:4], R_C)
    sums = csum[...] + csr[1] + csr[2] + csr[3]
    h_out = []
    for gi in (0, 1):
        hs[gi] = sums[:, gi * SLOTS : (gi + 1) * SLOTS]
    for gi in (0, 1):
        for cd in (0, 1):
            cp = remote(
                hs.at[gi], hsr.at[y], h_s.at[gi, cd], h_r.at[y],
                (z * 4 + 2 * c + gi, 2 * x + cd),
            )
            mine = jnp.logical_and(y == 2 * c + gi, c == cd)
            h_out.append((cp, mine))

            @pl.when(jnp.logical_not(mine))
            def _():
                cp.start()

            @pl.when(mine)
            def _():
                hsr[y] = hs[gi]

    arrived(frecv.at[1:4], R_F)
    out_ref[...] = (
        fown[...] + frecv[1].astype(F32) + frecv[2].astype(F32) + frecv[3].astype(F32)
    ).astype(BF)

    for src in range(4):
        @pl.when(jnp.logical_not(jnp.logical_and(src == y, y // 2 == c)))
        def _():
            remote(hs.at[0], hsr.at[src], h_s.at[0, 0], h_r.at[src], peer).wait_recv()

    hm_ref[...] = (hsr[0] + hsr[1] + hsr[2] + hsr[3])[0:1, :] / TOKENS

    gone(kvb.at[0:3], S_KV)
    gone(qb.at[0:2], S_Q)
    gone(drow.at[0:3], S_DK)
    gone(drow.at[0:2], S_DQ)
    gone(orecv, S_O)
    gone(att.at[c], S_A)
    gone(wo.at[:, rows_c, :], S_WO)
    gone(psend.at[0:3], S_P)
    gone(wou.at[0 : 3 * SLOTS], S_WU)
    gone(sqs.at[1:8], S_SQ)
    gone(inv_row.at[1:4], S_IV)
    gone(fsend.at[1:4], S_N)
    gone(nb.at[0:2], S_ND)
    gone(ab.at[0:3], S_X)
    gone(presend, S_AD)
    gone(fsend.at[1:4], S_F)
    gone(csr.at[1:4], S_C)
    for cp, mine in h_out:
        @pl.when(jnp.logical_not(mine))
        def _():
            cp.wait_send()

    @pl.when(ct != c)
    def _():
        wi_peer.wait_send()

    for cp in wi_out:
        cp.wait_send()
    for j in (0, 1):
        here, cp = pass_in(j)

        @pl.when(here)
        def _():
            cp.wait_send()


def local(resid, queries, keys, values, doc_ids, out_proj, ffn_gain, w_in, w_out, hot_index,
          hot_blocks):
    dma = pltpu.SemaphoreType.DMA
    V = pltpu.VMEM
    hbm = pl.BlockSpec(memory_space=pl.ANY)
    vm = pl.BlockSpec(memory_space=pltpu.VMEM)
    sm = pl.BlockSpec(memory_space=pltpu.SMEM)
    scratch = [
        V((3, HEADS, TOK, 128), BF), V((4, HEADS, 2, TOK, 128), BF),
        V((4, 8, TOK), F32), V((3, 8, TOK), F32), V((4, TOK, 128), F32),
        V((HEADS, 128, TOK), F32), V((HEADS, 8, TOK), F32),
        V((2, HEADS, 144, TOK), BF), V((2, HEADS, 8, TOK), F32),
        V((2, HEADS, 144, TOK), BF), V((2, HEADS, 8, TOK), F32),
        V((2, HEADS, TOK, 128), BF), V((4, 2 * WID, WID), BF), V((TOK, WID), BF),
        V((4, TOK, WID), BF), V((2, 2, 128, WID), BF), V((2, 2, 64, WID), BF), V((2, TOK, WID), F32),
        V((NEUR, WID), BF), V((NEUR, WID), BF), V((WID, SLOTS), BF),
        V((2 * WID, 2 * SLOTS), BF), V((4 * SLOTS, WID), BF),
        V((8, 8, TOK), F32), V((4, 8, TOK), F32), V((4, TOK, 128), F32), V((4, 2, TOK, WID), BF),
        V((4, TOK, 2 * SLOTS), F32),
        V((4, TOK, 2 * SLOTS), BF), V((8, 3, 32, 2 * SLOTS), BF), V((8, 2, 16, 2 * SLOTS), BF),
        V((8, 2, 16, 2 * SLOTS), BF), V((4, 2, TOK, 2 * SLOTS), BF),
        V((TOK, WID), F32), V((4, TOK, WID), BF), V((4, TOK, WID), BF),
        V((8, 2 * SLOTS), F32), V((4, 8, 2 * SLOTS), F32), V((2, 8, SLOTS), F32),
        V((4, 8, SLOTS), F32),
        dma((17,)), dma((3, HEADS)), dma((HEADS,)), dma((HEADS,)), dma((4,)), dma((3,)), dma((2,)),
        dma((6,)), dma((2, 2)), dma((3, 2)), dma((4, 2)), dma((8,)), dma((8,)), dma((8,)),
        dma((8,)), dma((8,)), dma((11,)), dma((2, 2)), dma((4,)),
    ]
    return pl.pallas_call(
        kernel,
        out_shape=(
            jax.ShapeDtypeStruct((TOK, WID), BF), jax.ShapeDtypeStruct((1, SLOTS), F32),
        ),
        in_specs=[hbm, hbm, hbm, hbm, vm, hbm, vm, hbm, hbm, vm, sm],
        out_specs=(vm, vm),
        scratch_shapes=scratch,
        compiler_params=pltpu.CompilerParams(
            collective_id=0, has_side_effects=True, vmem_limit_bytes=60 * 2**20
        ),
        name="layer",
    )(
        queries, keys, values, resid, doc_ids.reshape(1, TOK), out_proj,
        ffn_gain, w_in.T, w_out, hot_index, hot_blocks,
    )


def solution(mesh):
    return jax.shard_map(
        local,
        mesh=mesh,
        in_specs=(
            P("seq", "mp"), P("seq", "mp"), P("seq", "mp"), P("seq", "mp"), P("seq"),
            P("mp", None), P("mp"), P("mp", "seq"), P("seq", "mp"), P("seq", None), P("seq"),
        ),
        out_specs=(P("seq", "mp"), P("seq", None)),
        check_vma=False,
    )
```

time: 136 us -> 107 us (0.79)
  the two profiles are of different devices: /device:TPU:15 before, /device:TPU:1 now
where the time goes in v3:
time: 107 us; the launch traced here: 106 us
  Pallas kernels  102 us (95%)
  local copies, waits for them, and re-layouts  2.97 us (3%)
  between operations  1.29 us (1%)
    pallas_call x1, Pallas kernels, local(): pl.pallas_call(kernel, out_shape=(jax.ShapeDtypeStruct((TOK, WID), BF), j...  102 us
    unnamed x2, local copies, waits for them, and re-layouts  2.97 us

profile of v3, /device:TPU:1, one launch (start us, length us, event | category | flops | bytes accessed | tf_op | source)
XLA Modules:
  0.0 106.3 jit_solution(14428660097323119187)
XLA Ops:
  1.3 102.1 %layer.1 = (bf16[256,640]{1,0:T(8,128)(2,1)}, f32[1,384]{1,0:T(1,128)}) custom-call(bf16[256,640]{1,0:T(8,128)(2,1)} %q_ref.1, bf16[256,640]{1,0:T(8,128)(2,1)} %k_ref.1, bf16[256,640]{1,0:T(8,128)(2,1)} %v_ref.1, bf16[256,640]{1,0:T(8,128)(2,1)} %resid_ref.1, s32[1,256]{1,0:T(1,128)} %bitcast.3, bf16[640,5120]{1,0:T(8,128)(2,1)} %oproj_ref.1, ...), custom_call_target="tpu_custom_call" | custom-call | tf_op jit(solution)/shard_map/layer/pallas_call | solution.py:679
  103.4 1.7 %copy.16 = bf16[256,640]{1,0:T(8,128)(2,1)} copy(bf16[256,640]{1,0:T(8,128)(2,1)} %get-tuple-element.4) | data formatting | bytes 655360
  105.1 1.2 %copy.17 = f32[1,384]{1,0:T(1,128)} copy(f32[1,384]{1,0:T(1,128)} %get-tuple-element.5) | data formatting | bytes 3072

commit v4 on v3

--- a/solution.py
+++ b/solution.py
@@ -22,10 +22,11 @@
 F32 = jnp.float32
 ORDER = (1, 3, 2)
 PLAN = (
-    "t4", "b0", "s0", "t5", "t6", "r0", "t3", "a2", "b1", "a7", "n0", "c0", "b2", "b7", "r1",
-    "a4", "d0", "b4", "r2", "r7", "a5", "c1", "g0", "w0", "b5", "a3", "a6", "c2", "c4", "c7",
-    "b3", "d1", "r5", "b6", "d2", "g4", "d7", "r3", "e4", "g1", "c5", "r6", "e0", "e1", "g2",
-    "g7", "c3", "e2", "d5", "c6", "h0", "e7", "d3", "g5", "d6", "e5", "g3", "g6", "e3", "e6",
+    "b0", "s0", "t7", "t6", "r0", "a2", "a3", "b1", "n0", "c0", "b2", "b3", "r1", "a7", "a6",
+    "d0", "b7", "a4", "r2", "b6", "r3", "b4", "g0", "c1", "a5", "r7", "c2", "r6", "b5", "c3",
+    "w0", "r4", "d1", "c7", "d2", "c6", "r5", "d3", "c4", "g1", "d7", "e0", "e1", "g2", "d6",
+    "c5", "h0", "g3", "e2", "d4", "e3", "g6", "g7", "d5", "g4", "e6", "e7", "e4", "g5", "e5",
+    "q2", "q3", "q6", "q7",
 )
 
 
@@ -38,9 +39,9 @@
     hblk_ref, out_ref, hm_ref,
     qb, kvb, drow, qrow, kcol, acc0, st0, osend, ssend, orecv, srecv, att, wo, res,
     psend, precv, prel, pnear, wi_own, wo_own, hin, win, wou, sqs, inv_row, inv_col, nb, prebuf,
-    presend, prerecv, relrecv, relsend, ab, fown, fsend, frecv, csum, csr, hs, hsr,
+    presend, prerecv, relrecv, relsend, ab, fown, fsend, frecv, frel, fpart, csum, csr, hs, hsr,
     out_s, kv_r, q_r, o_r, p_r, l_s, own_l, wi_s, wi_r, n_r, nd_r, rel_r, rs_r, ag_r, fwd_r, ad_r,
-    one_r, h_s, h_r,
+    fr_r, one_r, h_s, h_r,
 ):
     s = lax.axis_index("seq")
     m = lax.axis_index("mp")
@@ -123,8 +124,8 @@
         if h < 2:
             for cp in direct(h):
                 cp.start()
-        for cp in ask(h):
-            cp.start()
+        for r, cp in zip((1, 2), ask(h)):
+            pl.when(z >= r)(cp.start)
 
     rows_c = pl.ds(pl.multiple_of(c * WID, 128), WID)
 
@@ -185,6 +186,19 @@
         g = (left, right)[j]
         part = wou.at[pl.ds(pl.multiple_of(g * SLOTS + j * (SLOTS // 2), 64), SLOTS // 2)]
         return remote(part, part, S_WU, R_WP, dev(dy=(1, 3)[j]))
+
+    def both(top, total):
+        row = lax.broadcasted_iota(jnp.int32, (8, TOK), 0)
+        return jnp.where(row == 0, top, total)
+
+    for i in (1, 2):
+
+        @pl.when(z < i)
+        def _():
+            orecv[i - 1] = jnp.zeros_like(orecv[i - 1])
+            srecv[i - 1] = jnp.broadcast_to(
+                both(jnp.full((1, TOK), LOW, F32), jnp.zeros((1, TOK), F32)), (HEADS, 8, TOK)
+            )
 
     choose()
     arrived(drow.at[1:4], R_DK)
@@ -217,10 +231,6 @@
             acc = acc + mixed * factor
         return top, total, acc
 
-    def both(top, total):
-        row = lax.broadcasted_iota(jnp.int32, (8, TOK), 0)
-        return jnp.where(row == 0, top, total)
-
     def back(i, h):
         return (
             remote(
@@ -239,7 +249,14 @@
             for cp in direct(h + 2):
                 cp.start()
 
-        arrived(qb.at[1:3, h], q_r.at[h])
+        @pl.when(z <= 1)
+        def _():
+            arrived(qb.at[1:3, h], q_r.at[h])
+
+        @pl.when(z == 2)
+        def _():
+            arrived(qb.at[1, h], q_r.at[h])
+
         q0 = qrow[0][0:1, :]
         q1 = jnp.where(z + 1 <= 3, qrow[1][0:1, :], -5.0)
         q2 = jnp.where(z + 2 <= 3, qrow[2][0:1, :], -5.0)
@@ -279,8 +296,12 @@
             top, total, acc = together(parts_of)
             osend[i - 1, h, 0:128] = acc.astype(BF)
             ssend[i - 1, h] = both(top, total)
-            for cp in back(i, h):
-                cp.start()
+
+            @pl.when(z + i <= 3)
+            def _():
+                for cp in back(i, h):
+                    cp.start()
+
         top, total, acc = together(
             [mix[0]] + [(jnp.where(n <= y, mix[n][0], LOW), mix[n][1], mix[n][2]) for n in (1, 2, 3)]
         )
@@ -307,7 +328,14 @@
         return remote(att.at[c, h], att.at[c, h], S_A, R_A, peer)
 
     def merge(h, _):
-        arrived(orecv.at[:, h], o_r.at[h])
+        @pl.when(z >= 2)
+        def _():
+            arrived(orecv.at[:, h], o_r.at[h])
+
+        @pl.when(z == 1)
+        def _():
+            arrived(orecv.at[0, h], o_r.at[h])
+
         t0, t1, t2 = st0[h][0:1, :], srecv[0, h][0:1, :], srecv[1, h][0:1, :]
         n0, n1, n2 = st0[h][1:2, :], srecv[0, h][1:2, :], srecv[1, h][1:2, :]
         top = jnp.maximum(t0, jnp.maximum(t1, t2))
@@ -370,9 +398,6 @@
             cp.wait_recv()
             cp.start()
 
-    for cp in wu_out:
-        cp.start()
-
     onward(0)
     beside(1)
     for k in (0, 1):
@@ -425,10 +450,10 @@
     csum[...] = jnp.zeros_like(csum)
     parts = tuple(
         (r, 128 * k, 128)
-        for r, k in ((0, 0), (0, 1), (1, 0), (3, 1), (2, 0), (2, 1), (1, 1), (3, 0))
+        for r, k in ((0, 0), (0, 1), (1, 0), (3, 0), (2, 0), (2, 1), (1, 1), (3, 1))
     )
 
-    plain = (4,)
+    plain = ()
 
     def quarter(b, at):
         _, first, n = parts[b]
@@ -452,10 +477,13 @@
         columns_of(0, inv_row[0][0:1, :])
 
     def stage_a(b):
-        r, first, _ = parts[b]
-        if r:
-            n_in[r, first // 128].wait_recv()
-            mate(r, first // 128)
+        r, first, n = parts[b]
+        k = first // 128
+        arrived(nb.at[r, c, first : first + n], n_r.at[r - 1, k])
+        mate(r, k)
+        if r != 2:
+            half = slice(first + 32 * (r - 1), first + 32 * (r - 1) + 64)
+            go(remote(nb.at[r, c, half], nb.at[2, c, half], S_N, n_r.at[1, k], dev(dz=r)))
 
     def stage_b(b):
         r, first, n = parts[b]
@@ -541,7 +569,7 @@
 
     def stage_e(b):
         r, first, n = parts[b]
-        if b == 4:
+        if b == 0:
             arrived(wou.at[0:SLOTS], R_WP)
         arrived(ab.at[r, 1 - c, first : first + n], ad_r.at[b])
         at = slice(first, first + n)
@@ -550,10 +578,33 @@
         if r == 0:
             fown[at] = part + res[at].astype(F32)
         else:
-            fsend[r, at] = part.astype(BF)
-            go(remote(fsend.at[r, at], frecv.at[r, at], S_F, R_F, dev(dz=-r)))
+            k = first // 128
+            for j, e in ((0, 3), (1, 1)):
+                mine = slice(64 * j, 64 * j + 64)
+                there = slice(first + 64 * j, first + 64 * j + 64)
+                if r == 2:
+                    fsend[r, there] = part[mine].astype(BF)
+                    go(remote(fsend.at[r, there], frel.at[k, j], S_F, fr_r.at[k, j], dev(dz=e)))
+                elif r == e:
+                    fsend[r, there] = part[mine].astype(BF)
+                    home(r, there)
+                else:
+                    fpart[k, j] = part[mine]
+
+    def home(r, rows):
+        go(remote(fsend.at[r, rows], frecv.at[r // 2, rows], S_F, R_F, dev(dz=-r)))
+
+    def stage_q(b):
+        r, first, n = parts[b]
+        k, j = first // 128, r // 2
+        arrived(frel.at[k, j], fr_r.at[k, j])
+        rows = slice(first + 64 * j, first + 64 * j + 64)
+        fsend[r, rows] = (fpart[k, j] + frel[k, j].astype(F32)).astype(BF)
+        home(r, rows)
 
     def stage_s(b):
+        for cp in wu_out:
+            cp.start()
         settle(1)
         wide = res[...].astype(F32)
         square = wide * wide
@@ -574,6 +625,7 @@
     stage = {
         "n": stage_n, "a": stage_a, "b": stage_b, "r": stage_r, "c": stage_c, "d": stage_d,
         "g": stage_g, "e": stage_e, "h": stage_h, "s": stage_s, "t": stage_t, "w": stage_w,
+        "q": stage_q,
     }
     for word in PLAN:
         stage[word[0]](int(word[1]))
@@ -600,9 +652,9 @@
             def _():
                 hsr[y] = hs[gi]
 
-    arrived(frecv.at[1:4], R_F)
+    arrived(frecv, R_F)
     out_ref[...] = (
-        fown[...] + frecv[1].astype(F32) + frecv[2].astype(F32) + frecv[3].astype(F32)
+        fown[...] + frecv[0].astype(F32) + frecv[1].astype(F32)
     ).astype(BF)
 
     for src in range(4):
@@ -613,10 +665,24 @@
     hm_ref[...] = (hsr[0] + hsr[1] + hsr[2] + hsr[3])[0:1, :] / TOKENS
 
     gone(kvb.at[0:3], S_KV)
-    gone(qb.at[0:2], S_Q)
+    @pl.when(z >= 2)
+    def _():
+        gone(qb.at[0:2], S_Q)
+
+    @pl.when(z == 1)
+    def _():
+        gone(qb.at[0], S_Q)
+
+    @pl.when(z <= 1)
+    def _():
+        gone(orecv, S_O)
+
+    @pl.when(z == 2)
+    def _():
+        gone(orecv.at[0], S_O)
+
     gone(drow.at[0:3], S_DK)
     gone(drow.at[0:2], S_DQ)
-    gone(orecv, S_O)
     gone(att.at[c], S_A)
     gone(wo.at[:, rows_c, :], S_WO)
     gone(psend.at[0:3], S_P)
@@ -646,6 +712,11 @@
         @pl.when(here)
         def _():
             cp.wait_send()
+
+
+def finish(layer_ref, mean_ref, out_ref, hm_ref):
+    out_ref[...] = layer_ref[...]
+    hm_ref[...] = mean_ref[...]
 
 
 def local(resid, queries, keys, values, doc_ids, out_proj, ffn_gain, w_in, w_out, hot_index,
@@ -669,14 +740,15 @@
         V((4, TOK, 2 * SLOTS), F32),
         V((4, TOK, 2 * SLOTS), BF), V((8, 3, 32, 2 * SLOTS), BF), V((8, 2, 16, 2 * SLOTS), BF),
         V((8, 2, 16, 2 * SLOTS), BF), V((4, 2, TOK, 2 * SLOTS), BF),
-        V((TOK, WID), F32), V((4, TOK, WID), BF), V((4, TOK, WID), BF),
+        V((TOK, WID), F32), V((4, TOK, WID), BF), V((2, TOK, WID), BF), V((2, 2, 64, WID), BF),
+        V((2, 2, 64, WID), F32),
         V((8, 2 * SLOTS), F32), V((4, 8, 2 * SLOTS), F32), V((2, 8, SLOTS), F32),
         V((4, 8, SLOTS), F32),
         dma((17,)), dma((3, HEADS)), dma((HEADS,)), dma((HEADS,)), dma((4,)), dma((3,)), dma((2,)),
         dma((6,)), dma((2, 2)), dma((3, 2)), dma((4, 2)), dma((8,)), dma((8,)), dma((8,)),
-        dma((8,)), dma((8,)), dma((11,)), dma((2, 2)), dma((4,)),
+        dma((8,)), dma((8,)), dma((2, 2)), dma((11,)), dma((2, 2)), dma((4,)),
     ]
-    return pl.pallas_call(
+    layer, mean = pl.pallas_call(
         kernel,
         out_shape=(
             jax.ShapeDtypeStruct((TOK, WID), BF), jax.ShapeDtypeStruct((1, SLOTS), F32),
@@ -692,6 +764,11 @@
         queries, keys, values, resid, doc_ids.reshape(1, TOK), out_proj,
         ffn_gain, w_in.T, w_out, hot_index, hot_blocks,
     )
+    return pl.pallas_call(
+        finish, out_shape=(
+            jax.ShapeDtypeStruct((TOK, WID), BF), jax.ShapeDtypeStruct((1, SLOTS), F32),
+        ), in_specs=[vm, vm], out_specs=(vm, vm), name="finish",
+    )(layer, mean)
 
 
 def solution(mesh):

time: 107 us -> 102 us (0.953)
  local copies, waits for them, and re-layouts: 2.97 us -> 0 us
    unnamed x2 -> x0, local copies, waits for them, and re-layouts: 2.97 us -> none
    pallas_call x1, Pallas kernels: 102 us -> 99.2 us  [local(): pl.pallas_call(kernel, out_shape=(jax.ShapeDtypeStruct((TOK, WID), BF), j...]
    pallas_call x0 -> x1, Pallas kernels: none -> 1.73 us  [local(): pl.pallas_call(finish, out_shape=(jax.ShapeDtypeStruct((TOK, WID), BF), j...]
where the time goes in v4:
time: 102 us
  Pallas kernels  101 us (99%)
  between operations  1.29 us (1%)
    pallas_call x1, Pallas kernels, local(): pl.pallas_call(kernel, out_shape=(jax.ShapeDtypeStruct((TOK, WID), BF), j...  99.2 us

profile of v4, /device:TPU:1, one launch (start us, length us, event | category | flops | bytes accessed | tf_op | source)
XLA Modules:
  0.0 102.2 jit_solution(11552387926928795857)
XLA Ops:
  1.3 99.2 %layer.1 = (bf16[256,640]{1,0:T(8,128)(2,1)}, f32[1,384]{1,0:T(1,128)}) custom-call(bf16[256,640]{1,0:T(8,128)(2,1)} %q_ref.1, bf16[256,640]{1,0:T(8,128)(2,1)} %k_ref.1, bf16[256,640]{1,0:T(8,128)(2,1)} %v_ref.1, bf16[256,640]{1,0:T(8,128)(2,1)} %resid_ref.1, s32[1,256]{1,0:T(1,128)} %bitcast.3, bf16[640,5120]{1,0:T(8,128)(2,1)} %oproj_ref.1, ...), custom_call_target="tpu_custom_call" | custom-call | tf_op jit(solution)/shard_map/layer/pallas_call | solution.py:751
  100.5 1.7 %finish.1 = (bf16[256,640]{1,0:T(8,128)(2,1)}, f32[1,384]{1,0:T(1,128)}) custom-call(bf16[256,640]{1,0:T(8,128)(2,1)} %get-tuple-element.4.layer_ref, f32[1,384]{1,0:T(1,128)} %get-tuple-element.5.mean_ref), custom_call_target="tpu_custom_call" | custom-call | tf_op jit(solution)/shard_map/finish/pallas_call | solution.py:767

commit v5 on v4

--- a/solution.py
+++ b/solution.py
@@ -23,10 +23,10 @@
 ORDER = (1, 3, 2)
 PLAN = (
     "b0", "s0", "t7", "t6", "r0", "a2", "a3", "b1", "n0", "c0", "b2", "b3", "r1", "a7", "a6",
-    "d0", "b7", "a4", "r2", "b6", "r3", "b4", "g0", "c1", "a5", "r7", "c2", "r6", "b5", "c3",
-    "w0", "r4", "d1", "c7", "d2", "c6", "r5", "d3", "c4", "g1", "d7", "e0", "e1", "g2", "d6",
-    "c5", "h0", "g3", "e2", "d4", "e3", "g6", "g7", "d5", "g4", "e6", "e7", "e4", "g5", "e5",
-    "q2", "q3", "q6", "q7",
+    "d0", "a4", "r2", "b4", "r3", "b6", "c1", "g0", "a5", "c2", "r4", "b5", "w0", "c3", "d1",
+    "r6", "b7", "d2", "c4", "r5", "d3", "g1", "c6", "e0", "e1", "g2", "r7", "d4", "c5", "g3",
+    "e2", "d6", "c7", "h0", "e3", "g4", "d5", "g6", "e4", "d7", "e6", "g5", "q2", "e5", "q3",
+    "g7", "e7", "q6", "q7",
 )
 
 
@@ -37,7 +37,7 @@
 def kernel(
     q_ref, k_ref, v_ref, resid_ref, doc_ref, oproj_ref, gain_ref, win_ref, wout_ref, hidx_ref,
     hblk_ref, out_ref, hm_ref,
-    qb, kvb, drow, qrow, kcol, acc0, st0, osend, ssend, orecv, srecv, att, wo, res,
+    doc_here, gain_here, hidx_here, qb, kvb, drow, qrow, kcol, acc0, st0, osend, ssend, orecv, srecv, att, wo, res,
     psend, precv, prel, pnear, wi_own, wo_own, hin, win, wou, sqs, inv_row, inv_col, nb, prebuf,
     presend, prerecv, relrecv, relsend, ab, fown, fsend, frecv, frel, fpart, csum, csr, hs, hsr,
     out_s, kv_r, q_r, o_r, p_r, l_s, own_l, wi_s, wi_r, n_r, nd_r, rel_r, rs_r, ag_r, fwd_r, ad_r,
@@ -86,7 +86,12 @@
         pltpu.make_async_copy(wout_ref, wo_own, l_s.at[1]),
         pltpu.make_async_copy(resid_ref, res, l_s.at[2]),
     ]
-    for cp in big:
+    small = [
+        pltpu.make_async_copy(doc_ref, doc_here, l_s.at[3]),
+        pltpu.make_async_copy(gain_ref, gain_here, l_s.at[4]),
+        pltpu.make_async_copy(hidx_ref, hidx_here, l_s.at[5]),
+    ]
+    for cp in small + big:
         cp.start()
 
     barrier = pltpu.get_barrier_semaphore()
@@ -95,9 +100,11 @@
         friends += [dev(dy=r), dev(dy=r, dc=1), dev(dz=r), dev(dx=r), dev(dx=r, dc=1)]
     for f in friends:
         pl.semaphore_signal(barrier, inc=1, device_id=f, device_id_type=pl.DeviceIdType.MESH)
-    doc_here = jnp.broadcast_to(doc_ref[...].astype(F32), (8, TOK))
-    drow[0] = doc_here
-    qrow[0] = doc_here
+    for cp in small:
+        cp.wait()
+    documents = jnp.broadcast_to(doc_here[...].astype(F32), (8, TOK))
+    drow[0] = documents
+    qrow[0] = documents
     pl.semaphore_wait(barrier, len(friends))
     for r in (1, 2, 3):
         go(remote(drow.at[0], drow.at[r], S_DK, R_DK, dev(dy=r)))
@@ -154,7 +161,7 @@
         for cp in big:
             cp.wait()
         live = lax.broadcasted_iota(jnp.int32, (1, SLOTS), 1) < BLOCK * hblk_ref[0]
-        want = jnp.where(live, hidx_ref[...], -1)
+        want = jnp.where(live, hidx_here[...], -1)
         pick = (lax.broadcasted_iota(jnp.int32, (NEUR, SLOTS), 0) == want).astype(F32).astype(BF)
         hin[...] = dot(wi_own[...], pick, ((0,), (0,))).astype(BF)
         wou[my_rows, :] = dot(pick, wo_own[...], ((0,), (0,))).astype(BF)
@@ -271,12 +278,14 @@
         near, mix = {}, {}
         for n in (0, 1, 3):
             near[n] = pair(h, 1, n, q1)
-        for n in (0, 1, 4):
+        mix[0] = shared(0)
+
+        @pl.when(h + 1 < HEADS)
+        def _():
+            pass_on(h + 1)
+
+        for n in (1, 4):
             mix[n] = shared(n)
-
-        @pl.when(h + 1 < HEADS)
-        def _():
-            pass_on(h + 1)
 
         @pl.when(h == HEADS - 2)
         def _():
@@ -417,7 +426,7 @@
         half = nb.at[r, c, 128 * k : 128 * k + 128]
         nd_in[r, k] = go(remote(half, half, S_ND, nd_r.at[r, k], peer))
 
-    gain = gain_ref[...].astype(F32).reshape(1, WID)
+    gain = gain_here[...].astype(F32).reshape(1, WID)
 
     def settle(k):
         at = slice(128 * k, 128 * k + 128)
@@ -727,6 +736,7 @@
     vm = pl.BlockSpec(memory_space=pltpu.VMEM)
     sm = pl.BlockSpec(memory_space=pltpu.SMEM)
     scratch = [
+        V((1, TOK), jnp.int32), V((WID,), BF), V((1, SLOTS), jnp.int32),
         V((3, HEADS, TOK, 128), BF), V((4, HEADS, 2, TOK, 128), BF),
         V((4, 8, TOK), F32), V((3, 8, TOK), F32), V((4, TOK, 128), F32),
         V((HEADS, 128, TOK), F32), V((HEADS, 8, TOK), F32),
@@ -744,7 +754,7 @@
         V((2, 2, 64, WID), F32),
         V((8, 2 * SLOTS), F32), V((4, 8, 2 * SLOTS), F32), V((2, 8, SLOTS), F32),
         V((4, 8, SLOTS), F32),
-        dma((17,)), dma((3, HEADS)), dma((HEADS,)), dma((HEADS,)), dma((4,)), dma((3,)), dma((2,)),
+        dma((17,)), dma((3, HEADS)), dma((HEADS,)), dma((HEADS,)), dma((4,)), dma((6,)), dma((2,)),
         dma((6,)), dma((2, 2)), dma((3, 2)), dma((4, 2)), dma((8,)), dma((8,)), dma((8,)),
         dma((8,)), dma((8,)), dma((2, 2)), dma((11,)), dma((2, 2)), dma((4,)),
     ]
@@ -753,7 +763,7 @@
         out_shape=(
             jax.ShapeDtypeStruct((TOK, WID), BF), jax.ShapeDtypeStruct((1, SLOTS), F32),
         ),
-        in_specs=[hbm, hbm, hbm, hbm, vm, hbm, vm, hbm, hbm, vm, sm],
+        in_specs=[hbm] * 10 + [sm],
         out_specs=(vm, vm),
         scratch_shapes=scratch,
         compiler_params=pltpu.CompilerParams(

time: 102 us -> 102 us (level)
  no operation moved by 1% of the time
where the time goes in v5:
time: 102 us
  Pallas kernels  100 us (98%)
  between operations  1.29 us (1%)
    pallas_call x1, Pallas kernels, local(): pl.pallas_call(kernel, out_shape=(jax.ShapeDtypeStruct((TOK, WID), BF), j...  98.6 us

profile of v5, /device:TPU:1, one launch (start us, length us, event | category | flops | bytes accessed | tf_op | source)
XLA Modules:
  0.0 101.7 jit_solution(2304153062109757640)
XLA Ops:
  1.3 98.6 %layer.1 = (bf16[256,640]{1,0:T(8,128)(2,1)}, f32[1,384]{1,0:T(1,128)}) custom-call(bf16[256,640]{1,0:T(8,128)(2,1)} %q_ref.1, bf16[256,640]{1,0:T(8,128)(2,1)} %k_ref.1, bf16[256,640]{1,0:T(8,128)(2,1)} %v_ref.1, bf16[256,640]{1,0:T(8,128)(2,1)} %resid_ref.1, s32[1,256]{1,0:T(1,128)} %bitcast.3, bf16[640,5120]{1,0:T(8,128)(2,1)} %oproj_ref.1, ...), custom_call_target="tpu_custom_call" | custom-call | tf_op jit(solution)/shard_map/layer/pallas_call | solution.py:761
  99.9 1.7 %finish.1 = (bf16[256,640]{1,0:T(8,128)(2,1)}, f32[1,384]{1,0:T(1,128)}) custom-call(bf16[256,640]{1,0:T(8,128)(2,1)} %get-tuple-element.4.layer_ref, f32[1,384]{1,0:T(1,128)} %get-tuple-element.5.mean_ref), custom_call_target="tpu_custom_call" | custom-call | tf_op jit(solution)/shard_map/finish/pallas_call | solution.py:777
